TPU v7x, 32 devices: a 4x4x1 block of a 4x4x8 slice. The times are simulated.
32 devices in a mesh: data: 1 (over z), expert: 32 (over y, x, core).
Axes of the slice: x: 4, y: 4, z: 1, core: 2. Of those that a mesh axis runs over, the one named last changes fastest.
The devices are a block of a 4x4x8 slice.
Arguments:
- x_a: bfloat16 [8192, 1024], P(('data', 'expert'))
- x_b: bfloat16 [8192, 1024], P(('data', 'expert'))
- dy_b: bfloat16 [8192, 1024], P(('data', 'expert'))
- eid_a: int32 [8192, 8], P(('data', 'expert'))
- slot_a: int32 [8192, 8], P(('data', 'expert'))
- gate_a: bfloat16 [8192, 8], P(('data', 'expert'))
- eid_b: int32 [8192, 8], P(('data', 'expert'))
- slot_b: int32 [8192, 8], P(('data', 'expert'))
- gate_b: bfloat16 [8192, 8], P(('data', 'expert'))
- u_b: bfloat16 [32, 4096, 1024], P(('data', 'expert'))
- norm_1: bfloat16 [1024], replicated
- norm_2: bfloat16 [1024], replicated
- w_q: bfloat16 [1024, 16, 64], replicated
- w_k: bfloat16 [1024, 8, 64], replicated
- w_v: bfloat16 [1024, 8, 64], replicated
- w_o: bfloat16 [16, 64, 1024], replicated
- w_1: bfloat16 [32, 1024, 512], P('expert')
- w_2: bfloat16 [32, 512, 1024], P('expert')
- w_3: bfloat16 [32, 1024, 512], P('expert')
Outputs:
- output 1: bfloat16 [8192, 1024], P(('data', 'expert'))
- output 2: bfloat16 [8192, 1024], P(('data', 'expert'))
- output 3: float32 [32, 1024, 512], P(('data', 'expert'))
- output 4: float32 [32, 512, 1024], P(('data', 'expert'))
- output 5: float32 [32, 1024, 512], P(('data', 'expert'))
- output 6: float32 [32, 1024, 16, 64], P(('data', 'expert'))
- output 7: float32 [32, 1024, 8, 64], P(('data', 'expert'))
- output 8: float32 [32, 1024, 8, 64], P(('data', 'expert'))
- output 9: float32 [32, 16, 64, 1024], P(('data', 'expert'))
- output 10: float32 [32, 1024], P(('data', 'expert'))
- output 11: float32 [32, 1024], P(('data', 'expert'))
All inputs are finite; a program needn't handle non-finite values.
Results may differ from a plain program's by a relative error of at most 0.0177277.
Values are sent between devices in bfloat16 or wider.
A program may use at most 768 MiB of HBM per device.

v0:
```python
import jax
import jax.numpy as jnp
from jax import lax
from jax.sharding import PartitionSpec as P

NORM_EPS = 1e-6


def rms_norm(values, gain):
    wide = values.astype(jnp.float32)
    scaled = wide * lax.rsqrt(jnp.mean(wide * wide, axis=-1, keepdims=True) + NORM_EPS)
    return (scaled * gain.astype(jnp.float32)).astype(jnp.bfloat16)


def add_rows(first, second):
    return (first.astype(jnp.float32) + second.astype(jnp.float32)).astype(jnp.bfloat16)


def attn_out(x_rows, norm_gain, w_q, w_k, w_v, w_o):
    tokens = x_rows.shape[0]
    heads = w_q.shape[1]
    kv_heads = w_k.shape[1]
    head_dim = w_q.shape[2]
    normed = rms_norm(x_rows, norm_gain)
    query = jnp.einsum('td,dhe->the', normed, w_q, preferred_element_type=jnp.float32).astype(jnp.bfloat16)
    query = query.reshape(tokens, kv_heads, heads // kv_heads, head_dim)
    key_proj = jnp.einsum('td,dge->tge', normed, w_k, preferred_element_type=jnp.float32).astype(jnp.bfloat16)
    val_proj = jnp.einsum('td,dge->tge', normed, w_v, preferred_element_type=jnp.float32).astype(jnp.bfloat16)
    scores = jnp.einsum('tgre,mge->grtm', query, key_proj, preferred_element_type=jnp.float32) * head_dim ** -0.5
    causal = jnp.arange(tokens)[:, None] >= jnp.arange(tokens)[None, :]
    scores = jnp.where(causal, scores, -1e30)
    probs = jax.nn.softmax(scores, axis=-1).astype(jnp.bfloat16)
    context = jnp.einsum('grtm,mge->tgre', probs, val_proj, preferred_element_type=jnp.float32).astype(jnp.bfloat16)
    context = context.reshape(tokens, heads, head_dim)
    return jnp.einsum('the,hed->td', context, w_o, preferred_element_type=jnp.float32).astype(jnp.bfloat16)


def dispatch(row_vals, expert_ids, slot_ids, experts, capacity):
    safe_slots = jnp.where(slot_ids >= 0, slot_ids, capacity)
    values = jnp.broadcast_to(row_vals, expert_ids.shape + (row_vals.shape[-1],))
    return jnp.zeros((experts, capacity, row_vals.shape[-1]), jnp.bfloat16).at[expert_ids, safe_slots].set(values, mode='drop')


def pick_rows(buf, expert_ids, slot_ids):
    safe_slots = jnp.where(slot_ids >= 0, slot_ids, buf.shape[1])
    return buf.at[expert_ids, safe_slots].get(mode='fill', fill_value=0)


def device_backward(x_dev, dy_dev, du_dev, norm_1, norm_2, w_q, w_k, w_v, w_o):
    attn_val, attn_pull = jax.vjp(attn_out, x_dev, norm_1, w_q, w_k, w_v, w_o)
    h_dev = add_rows(x_dev, attn_val)
    _, norm_pull = jax.vjp(rms_norm, h_dev, norm_2)
    dh_norm, grad_n2 = norm_pull(du_dev)
    dh_dev = add_rows(dy_dev, dh_norm)
    grad_x, grad_n1, grad_q, grad_k, grad_v, grad_o = attn_pull(dh_dev)
    return (add_rows(dh_dev, grad_x), grad_q.astype(jnp.float32), grad_k.astype(jnp.float32), grad_v.astype(jnp.float32), grad_o.astype(jnp.float32), grad_n1.astype(jnp.float32), grad_n2.astype(jnp.float32))


def solution(mesh):
    group = mesh.shape['expert']

    def local_step(x_a, x_b, dy_b, eid_a, slot_a, gate_a, eid_b, slot_b, gate_b, u_b, norm_1, norm_2, w_q, w_k, w_v, w_o, w_1, w_2, w_3):
        local_experts = w_1.shape[0]
        experts = local_experts * group
        capacity = u_b.shape[1] // group
        model_dim = x_a.shape[1]

        h_a = add_rows(x_a, attn_out(x_a, norm_1, w_q, w_k, w_v, w_o))
        u_a = rms_norm(h_a, norm_2)
        send_a = dispatch(u_a[:, None, :], eid_a, slot_a, experts, capacity).reshape(group, local_experts, capacity, model_dim)
        recv_a = lax.all_to_all(send_a, 'expert', 0, 0, tiled=True)
        act_1 = jnp.einsum('pecd,edf->pecf', recv_a, w_1, preferred_element_type=jnp.float32).astype(jnp.bfloat16).astype(jnp.float32)
        act_3 = jnp.einsum('pecd,edf->pecf', recv_a, w_3, preferred_element_type=jnp.float32).astype(jnp.bfloat16).astype(jnp.float32)
        hidden = (act_1 * jax.nn.sigmoid(act_1) * act_3).astype(jnp.bfloat16)
        out_a = jnp.einsum('pecf,efd->pecd', hidden, w_2, preferred_element_type=jnp.float32).astype(jnp.bfloat16)
        back_a = lax.all_to_all(out_a, 'expert', 0, 0, tiled=True).reshape(experts, capacity, model_dim)
        mixed = jnp.einsum('tk,tkd->td', gate_a, pick_rows(back_a, eid_a, slot_a), preferred_element_type=jnp.float32)
        y_a = (h_a.astype(jnp.float32) + mixed).astype(jnp.bfloat16)

        grad_rows = gate_b[:, :, None] * dy_b[:, None, :]
        send_b = dispatch(grad_rows, eid_b, slot_b, experts, capacity).reshape(group, local_experts, capacity, model_dim)
        d_out = lax.all_to_all(send_b, 'expert', 0, 0, tiled=True)
        saved = u_b.reshape(local_experts, group, capacity, model_dim)
        pre_1 = jnp.einsum('epcd,edf->pecf', saved, w_1, preferred_element_type=jnp.float32).astype(jnp.bfloat16).astype(jnp.float32)
        pre_3 = jnp.einsum('epcd,edf->pecf', saved, w_3, preferred_element_type=jnp.float32).astype(jnp.bfloat16).astype(jnp.float32)
        sigma = jax.nn.sigmoid(pre_1)
        silu_1 = pre_1 * sigma
        hid_b = (silu_1 * pre_3).astype(jnp.bfloat16)
        grad_w2 = jnp.einsum('pecf,pecd->efd', hid_b, d_out, preferred_element_type=jnp.float32)
        grad_hid = jnp.einsum('pecd,efd->pecf', d_out, w_2, preferred_element_type=jnp.float32).astype(jnp.bfloat16).astype(jnp.float32)
        grad_a1 = (grad_hid * pre_3 * sigma * (1.0 + pre_1 * (1.0 - sigma))).astype(jnp.bfloat16)
        grad_a3 = (grad_hid * silu_1).astype(jnp.bfloat16)
        grad_w1 = jnp.einsum('epcd,pecf->edf', saved, grad_a1, preferred_element_type=jnp.float32)
        grad_w3 = jnp.einsum('epcd,pecf->edf', saved, grad_a3, preferred_element_type=jnp.float32)
        grad_in = (jnp.einsum('pecf,edf->pecd', grad_a1, w_1, preferred_element_type=jnp.float32) + jnp.einsum('pecf,edf->pecd', grad_a3, w_3, preferred_element_type=jnp.float32)).astype(jnp.bfloat16)
        back_b = lax.all_to_all(grad_in, 'expert', 0, 0, tiled=True).reshape(experts, capacity, model_dim)
        du_rows = jnp.sum(pick_rows(back_b, eid_b, slot_b), axis=1, dtype=jnp.float32).astype(jnp.bfloat16)
        dx_b, g_q, g_k, g_v, g_o, g_n1, g_n2 = device_backward(x_b, dy_b, du_rows, norm_1, norm_2, w_q, w_k, w_v, w_o)
        return (y_a, dx_b, grad_w1, grad_w2, grad_w3, g_q[None], g_k[None], g_v[None], g_o[None], g_n1[None], g_n2[None])

    row_spec = P(('data', 'expert'), None)
    cube_spec = P(('data', 'expert'), None, None)
    quad_spec = P(('data', 'expert'), None, None, None)
    expert_spec = P('expert', None, None)
    in_specs = (row_spec, row_spec, row_spec, row_spec, row_spec, row_spec, row_spec, row_spec, row_spec, cube_spec, P(), P(), P(), P(), P(), P(), expert_spec, expert_spec, expert_spec)
    out_specs = (row_spec, row_spec, cube_spec, cube_spec, cube_spec, quad_spec, quad_spec, quad_spec, quad_spec, row_spec, row_spec)
    return jax.shard_map(local_step, mesh=mesh, in_specs=in_specs, out_specs=out_specs, check_vma=False)
```

profile of v0, /device:TPU:103, one launch (start us, length us, event | category | flops | bytes accessed | tf_op | source)
XLA Modules:
  0.0 672.1 jit_solution(5522880470918677512)
XLA Ops:
  6.2 15.3 %scatter_custom_fusion.1 = bf16[4096,1024]{1,0:T(8,128)(2,1)} fusion(s32[2048]{0:T(1024)S(1)} %reshape.282, bf16[]{:T(256)} %constant.40.clone.1, bf16[256,1024]{1,0:T(8,128)(2,1)} %param.21, bf16[256,8]{1,0:T(8,128)(2,1)S(1)} %copy.65), kind=kCustom, calls=%fused_computation.59 | custom fusion | flops 2097152 | bytes 8978434
  21.4 8.7 %all-to-all-start.2 = ((bf16[32,1,128,1024]{3,2,1,0:T(8,128)(2,1)}), bf16[32,1,128,1024]{3,2,1,0:T(8,128)(2,1)}, u32[]{:S(2)}, u32[]{:S(2)}) async-start(bf16[32,1,128,1024]{3,2,1,0:T(8,128)(2,1)} %bitcast.490), calls=%async_computation.2 | async-start | bytes 16777216 | tf_op jit(solution)/shard_map/all_to_all | solution.py:82
  30.2 10.3 %convolution_convert_fusion = bf16[512,32,128]{0,2,1:T(8,128)(2,1)} fusion(bf16[32,128,1024]{2,1,0:T(8,128)(2,1)} %bitcast.514, bf16[1,1024,512]{2,1,0:T(8,128)(2,1)} %param.35), kind=kOutput, calls=%fused_computation.79 | convolution fusion | flops 4297064448 | bytes 13631488 | tf_op jit(solution)/shard_map/epcd,edf->pecf/dot_general | solution.py:84
  40.5 9.4 %convolution_convert_fusion.1 = bf16[512,32,128]{0,2,1:T(8,128)(2,1)} fusion(bf16[32,128,1024]{2,1,0:T(8,128)(2,1)} %bitcast.515, bf16[1,1024,512]{2,1,0:T(8,128)(2,1)S(1)} %copy-done.41), kind=kOutput, calls=%fused_computation.80 | convolution fusion | flops 4297064448 | bytes 13631488 | tf_op jit(solution)/shard_map/epcd,edf->pecf/dot_general | solution.py:85
  49.9 93.5 %all-to-all-done.2 = bf16[32,1,128,1024]{3,2,1,0:T(8,128)(2,1)} async-done(((bf16[32,1,128,1024]{3,2,1,0:T(8,128)(2,1)}), bf16[32,1,128,1024]{3,2,1,0:T(8,128)(2,1)}, u32[]{:S(2)}, u32[]{:S(2)}) %all-to-all-start.2) | async-done | bytes 8388640 | tf_op jit(solution)/shard_map/all_to_all | solution.py:82
  143.4 8.3 %fusion.63 = bf16[32,128,512]{2,1,0:T(8,128)(2,1)S(1)} fusion(bf16[32,1,128,1024]{3,2,1,0:T(8,128)(2,1)} %all-to-all-done.2, bf16[1,512,1024]{2,1,0:T(8,128)(2,1)} %param.36), kind=kOutput, calls=%fused_computation.78 | convolution fusion | flops 4297064448 | bytes 13631488 | tf_op jit(solution)/shard_map/pecd,efd->pecf/dot_general | solution.py:90
  153.8 22.1 %fusion.42 = f32[32,128,1024]{2,1,0:T(8,128)} fusion(bf16[1,1024,512]{2,1,0:T(8,128)(2,1)S(1)} %copy-done.43, bf16[32,128,512]{2,1,0:T(8,128)(2,1)S(1)} %fusion.63, bf16[512,32,128]{0,2,1:T(8,128)(2,1)S(1)} %copy-done.48, bf16[512,32,128]{0,2,1:T(8,128)(2,1)S(1)} %copy-done.47), kind=kOutput, calls=%fused_computation.57 | convolution fusion | flops 4322230272 | bytes 30408704 | tf_op jit(solution)/shard_map/pecf,edf->pecd/dot_general | solution.py:95
  175.8 11.9 %fusion.27 = bf16[32,1,128,1024]{3,2,1,0:T(8,128)(2,1)} fusion(f32[32,128,1024]{2,1,0:T(8,128)} %fusion.42, bf16[1,1024,512]{2,1,0:T(8,128)(2,1)S(1)} %copy-done.42, bf16[32,128,512]{2,1,0:T(8,128)(2,1)} %copy-done.49, bf16[512,32,128]{0,2,1:T(8,128)(2,1)S(1)} %copy-done.47), kind=kOutput, calls=%fused_computation.39 | convolution fusion | flops 4320133120 | bytes 34603008 | tf_op jit(solution)/shard_map/pecf,edf->pecd/dot_general | solution.py:95
  187.8 4.0 all-to-all-start.3
  207.4 4.7 fusion.190
  217.5 86.8 %all-to-all-done.3 = bf16[32,1,128,1024]{3,2,1,0:T(8,128)(2,1)} async-done(((bf16[32,1,128,1024]{3,2,1,0:T(8,128)(2,1)}), bf16[32,1,128,1024]{3,2,1,0:T(8,128)(2,1)}, u32[]{:S(2)}, u32[]{:S(2)}) %all-to-all-start.3) | async-done | bytes 8388640 | tf_op jit(solution)/shard_map/all_to_all | solution.py:96
  304.3 40.8 %gather_fusion.1 = bf16[2048,1024]{1,0:T(8,128)(2,1)} fusion(bf16[32,128,1024]{2,1,0:T(8,128)(2,1)} %bitcast.67, s32[2048]{0:T(1024)S(1)} %reshape.270), kind=kCustom, calls=%fused_computation.1 | custom fusion | bytes 8404992 | tf_op jit(solution)/shard_map/gather | solution.py:46
  345.1 4.5 fusion.39
  351.4 15.0 %scatter_custom_fusion = bf16[4096,1024]{1,0:T(8,128)(2,1)} fusion(s32[2048]{0:T(1024)S(1)} %reshape.276, bf16[]{:T(256)} %constant.40.clone.1, bf16[256,1024]{1,0:T(8,128)(2,1)} %get-tuple-element.57), kind=kCustom, calls=%fused_computation.64 | custom fusion | bytes 8912898
  366.4 4.5 all-to-all-start
  373.3 14.2 %fusion.75 = f32[1,1024,512]{1,2,0:T(8,128)} fusion(bf16[32,128,1024]{2,1,0:T(8,128)(2,1)} %bitcast.516, bf16[32,128,512]{2,1,0:T(8,128)(2,1)} %copy-done.49, bf16[512,32,128]{0,2,1:T(8,128)(2,1)} %convolution_convert_fusion.1, bf16[512,32,128]{0,2,1:T(8,128)(2,1)} %convolution_convert_fusion), kind=kOutput, calls=%fused_computation.102 | convolution fusion | flops 4322230272 | bytes 23068672 | tf_op jit(solution)/shard_map/epcd,pecf->edf/dot_general | solution.py:93
  390.4 11.9 %convolution_bitcast_fusion = f32[1,1024,512]{1,2,0:T(8,128)} fusion(bf16[32,128,1024]{2,1,0:T(8,128)(2,1)} %bitcast.517, bf16[32,128,512]{2,1,0:T(8,128)(2,1)} %copy-done.49, bf16[512,32,128]{0,2,1:T(8,128)(2,1)} %convolution_convert_fusion), kind=kOutput, calls=%fused_computation.104 | convolution fusion | flops 4311744512 | bytes 18874368 | tf_op jit(solution)/shard_map/epcd,pecf->edf/dot_general | solution.py:94
  405.3 78.8 %all-to-all-done = bf16[32,1,128,1024]{3,2,1,0:T(8,128)(2,1)} async-done(((bf16[32,1,128,1024]{3,2,1,0:T(8,128)(2,1)}), bf16[32,1,128,1024]{3,2,1,0:T(8,128)(2,1)}, u32[]{:S(2)}, u32[]{:S(2)}) %all-to-all-start) | async-done | bytes 8388640 | tf_op jit(solution)/shard_map/all_to_all | solution.py:71
  484.2 10.2 %fusion.22 = bf16[32,128,512]{2,1,0:T(8,128)(2,1)} fusion(bf16[32,1,128,1024]{3,2,1,0:T(8,128)(2,1)} %all-to-all-done, bf16[1,1024,512]{2,1,0:T(8,128)(2,1)} %param.37), kind=kOutput, calls=%fused_computation.33 | convolution fusion | flops 4294967296 | bytes 13631488 | tf_op jit(solution)/shard_map/pecd,edf->pecf/dot_general | solution.py:73
  494.3 15.5 %convert_bitcast_fusion.2 = bf16[32,1,128,1024]{3,2,1,0:T(8,128)(2,1)} fusion(bf16[32,128,512]{2,1,0:T(8,128)(2,1)} %fusion.22, bf16[32,1,128,1024]{3,2,1,0:T(8,128)(2,1)} %all-to-all-done, bf16[1,512,1024]{2,1,0:T(8,128)(2,1)} %param.36, bf16[1,1024,512]{2,1,0:T(8,128)(2,1)} %param.35), kind=kOutput, calls=%fused_computation.37 | convolution fusion | flops 8613003264 | bytes 23068672 | tf_op jit(solution)/shard_map/pecf,efd->pecd/dot_general | solution.py:75
  509.9 4.1 all-to-all-start.1
  514.0 12.0 %fusion.78 = f32[1,512,1024]{2,1,0:T(8,128)} fusion(bf16[32,1,128,1024]{3,2,1,0:T(8,128)(2,1)} %all-to-all-done.2, bf16[512,32,128]{0,2,1:T(8,128)(2,1)} %convolution_convert_fusion.1, bf16[512,32,128]{0,2,1:T(8,128)(2,1)} %convolution_convert_fusion), kind=kOutput, calls=%fused_computation.103 | convolution fusion | flops 4311744512 | bytes 18874368 | tf_op jit(solution)/shard_map/pecf,pecd->efd/dot_general | solution.py:89
  547.0 79.3 %all-to-all-done.1 = bf16[32,1,128,1024]{3,2,1,0:T(8,128)(2,1)} async-done(((bf16[32,1,128,1024]{3,2,1,0:T(8,128)(2,1)}), bf16[32,1,128,1024]{3,2,1,0:T(8,128)(2,1)}, u32[]{:S(2)}, u32[]{:S(2)}) %all-to-all-start.1) | async-done | bytes 8388640 | tf_op jit(solution)/shard_map/all_to_all | solution.py:76
  626.3 41.0 %gather_fusion = bf16[2048,1024]{1,0:T(8,128)(2,1)} fusion(bf16[32,128,1024]{2,1,0:T(8,128)(2,1)} %bitcast.39, s32[2048]{0:T(1024)S(1)} %copy-done.1), kind=kCustom, calls=%fused_computation | custom fusion | bytes 8404992 | tf_op jit(solution)/shard_map/gather | solution.py:46
  (172 shorter events, 63.8 us)
Async XLA Ops:
  0.6 198.9 %copy-start = (bf16[1024,16,64]{0,2,1:T(8,128)(2,1)S(1)}, bf16[1024,16,64]{0,2,1:T(8,128)(2,1)}, u32[]{:S(2)}) copy-start(bf16[1024,16,64]{0,2,1:T(8,128)(2,1)} %param.31) | copy-start | bytes 6291460
  21.4 122.0 %all-to-all-start.2 = ((bf16[32,1,128,1024]{3,2,1,0:T(8,128)(2,1)}), bf16[32,1,128,1024]{3,2,1,0:T(8,128)(2,1)}, u32[]{:S(2)}, u32[]{:S(2)}) async-start(bf16[32,1,128,1024]{3,2,1,0:T(8,128)(2,1)} %bitcast.490), calls=%async_computation.2 | async-start | bytes 16777216 | tf_op jit(solution)/shard_map/all_to_all | solution.py:82
  30.2 10.4 %copy-start.41 = (bf16[1,1024,512]{2,1,0:T(8,128)(2,1)S(1)}, bf16[1,1024,512]{2,1,0:T(8,128)(2,1)}, u32[]{:S(2)}) copy-start(bf16[1,1024,512]{2,1,0:T(8,128)(2,1)} %param.37) | copy-start | bytes 3145732
  143.4 10.3 %copy-start.43 = (bf16[1,1024,512]{2,1,0:T(8,128)(2,1)S(1)}, bf16[1,1024,512]{2,1,0:T(8,128)(2,1)}, u32[]{:S(2)}) copy-start(bf16[1,1024,512]{2,1,0:T(8,128)(2,1)} %param.35) | copy-start | bytes 3145732
  143.4 10.3 %copy-start.47 = (bf16[512,32,128]{0,2,1:T(8,128)(2,1)S(1)}, bf16[512,32,128]{0,2,1:T(8,128)(2,1)}, u32[]{:S(2)}) copy-start(bf16[512,32,128]{0,2,1:T(8,128)(2,1)} %convolution_convert_fusion) | copy-start | bytes 12582916
  143.4 10.3 %copy-start.48 = (bf16[512,32,128]{0,2,1:T(8,128)(2,1)S(1)}, bf16[512,32,128]{0,2,1:T(8,128)(2,1)}, u32[]{:S(2)}) copy-start(bf16[512,32,128]{0,2,1:T(8,128)(2,1)} %convolution_convert_fusion.1) | copy-start | bytes 12582916
  153.8 22.1 %copy-start.42 = (bf16[1,1024,512]{2,1,0:T(8,128)(2,1)S(1)}, bf16[1,1024,512]{2,1,0:T(8,128)(2,1)}, u32[]{:S(2)}) copy-start(bf16[1,1024,512]{2,1,0:T(8,128)(2,1)} %param.37) | copy-start | bytes 3145732
  187.8 116.5 %all-to-all-start.3 = ((bf16[32,1,128,1024]{3,2,1,0:T(8,128)(2,1)}), bf16[32,1,128,1024]{3,2,1,0:T(8,128)(2,1)}, u32[]{:S(2)}, u32[]{:S(2)}) async-start(bf16[32,1,128,1024]{3,2,1,0:T(8,128)(2,1)} %fusion.27), calls=%async_computation.3 | async-start | bytes 16777216 | tf_op jit(solution)/shard_map/all_to_all | solution.py:96
  191.9 13.9 %copy-start.27 = (f32[1024]{0:T(1024)}, f32[1024]{0:T(1024)S(1)}, u32[]{:S(2)}) copy-start(f32[1024]{0:T(1024)S(1)} %convert_element_type.353) | copy-start | bytes 12292
  192.7 14.8 %copy-start.20 = (pred[256,256]{0,1:T(8,128)(4,1)}, pred[256,256]{0,1:T(8,128)(4,1)S(1)}, u32[]{:S(2)}) copy-start(pred[256,256]{0,1:T(8,128)(4,1)S(1)} %iota_compare_fusion.1) | copy-start | bytes 196612
  192.9 6.7 copy-start.36
  193.1 6.5 copy-start.34
  194.9 5.6 copy-start.16
  366.4 6.1 copy-start.38
  366.4 117.7 %all-to-all-start = ((bf16[32,1,128,1024]{3,2,1,0:T(8,128)(2,1)}), bf16[32,1,128,1024]{3,2,1,0:T(8,128)(2,1)}, u32[]{:S(2)}, u32[]{:S(2)}) async-start(bf16[32,1,128,1024]{3,2,1,0:T(8,128)(2,1)} %bitcast.489), calls=%async_computation | async-start | bytes 16777216 | tf_op jit(solution)/shard_map/all_to_all | solution.py:71
  509.9 116.4 %all-to-all-start.1 = ((bf16[32,1,128,1024]{3,2,1,0:T(8,128)(2,1)}), bf16[32,1,128,1024]{3,2,1,0:T(8,128)(2,1)}, u32[]{:S(2)}, u32[]{:S(2)}) async-start(bf16[32,1,128,1024]{3,2,1,0:T(8,128)(2,1)} %convert_bitcast_fusion.2), calls=%async_computation.1 | async-start | bytes 16777216 | tf_op jit(solution)/shard_map/all_to_all | solution.py:76
  514.0 12.7 %copy-start.9 = (bf16[16,64,1024]{2,1,0:T(8,128)(2,1)S(1)}, bf16[16,64,1024]{2,1,0:T(8,128)(2,1)}, u32[]{:S(2)}) copy-start(bf16[16,64,1024]{2,1,0:T(8,128)(2,1)} %param.34) | copy-start | bytes 6291460
  514.0 13.4 %copy-start.3 = (f32[8,256,256,2]{2,1,3,0:T(8,128)S(1)}, f32[8,256,256,2]{2,1,3,0:T(8,128)}, u32[]{:S(2)}) copy-start(f32[8,256,256,2]{2,1,3,0:T(8,128)} %copy-done.2) | copy-start | bytes 12582916
  514.0 13.4 %copy-start.21 = (pred[256,256]{0,1:T(8,128)(4,1)S(1)}, pred[256,256]{0,1:T(8,128)(4,1)}, u32[]{:S(2)}) copy-start(pred[256,256]{0,1:T(8,128)(4,1)} %copy-done.20) | copy-start | bytes 196612
  514.0 13.4 %copy-start.23 = (f32[256,512]{0,1:S(1)}, f32[256,512]{0,1}, u32[]{:S(2)}) copy-start(f32[256,512]{0,1} %copy-done.22) | copy-start | bytes 1572868
  514.0 13.4 %copy-start.25 = (f32[8,2,256]{2,1,0:T(2,128)S(1)}, f32[8,2,256]{2,1,0:T(2,128)}, u32[]{:S(2)}) copy-start(f32[8,2,256]{2,1,0:T(2,128)} %copy-done.24) | copy-start | bytes 49156
  544.6 81.7 %copy-start.1 = (s32[2048]{0:T(1024)S(1)}, s32[2048]{0:T(1024)}, u32[]{:S(2)}) copy-start(s32[2048]{0:T(1024)} %reshape.264) | copy-start | bytes 24580
  626.3 41.0 %copy-start.26 = (bf16[256,8,1]{1,2,0:T(2,128)(2,1)S(1)}, bf16[256,8,1]{1,2,0:T(2,128)(2,1)}, u32[]{:S(2)}) copy-start(bf16[256,8,1]{1,2,0:T(2,128)(2,1)} %copy.82) | copy-start | bytes 12292
  626.3 41.0 %copy-start.33 = (pred[256,8]{1,0:T(8,128)(4,1)S(1)}, pred[256,8]{1,0:T(8,128)(4,1)}, u32[]{:S(2)}) copy-start(pred[256,8]{1,0:T(8,128)(4,1)} %copy.59) | copy-start | bytes 6148
  (30 other events, 95.7 us)
where the time goes:
time: 679 us; the launch traced here: 672 us
  waiting for transfers between devices  338 us (50%)
  matrix products  161 us (24%)
  local copies, waits for them, and re-layouts  110 us (16%)
  other arithmetic  39.2 us (6%)
  starting transfers between devices  21.4 us (3%)
    all_to_all x1, waiting for transfers between devices, local_step(): d_out = lax.all_to_all(send_b, 'expert', 0, 0, tiled=True)  93.5 us
    all_to_all x1, waiting for transfers between devices, local_step(): lax.all_to_all(grad_in, 'expert', 0, 0, tiled=True)  86.8 us
    gather x2, local copies, waits for them, and re-layouts, pick_rows(): return buf.at[expert_ids, safe_slots].get(mode='fill', fill_value=0)  81.8 us
    all_to_all x1, waiting for transfers between devices, local_step(): lax.all_to_all(out_a, 'expert', 0, 0, tiled=True)  79.3 us
    all_to_all x1, waiting for transfers between devices, local_step(): recv_a = lax.all_to_all(send_a, 'expert', 0, 0, tiled=True)  78.8 us
    unnamed x109, local copies, waits for them, and re-layouts  26.6 us
    dot_general x1, matrix products, local_step(): jnp.einsum('pecf,edf->pecd', grad_a1, w_1, preferred_element_type=jnp.flo...  22.1 us
    unnamed x3, other arithmetic  16 us
  transfers between devices with their start and end apart: 4, of which 4 were waited for; matrix products, arithmetic and copies ran while one was open for 16% of the time, Pallas kernels for 0%

commit v1 on v0

v1 whole, which is shorter than its diff:
```python
import functools

import jax
import jax.numpy as jnp
from jax import lax
from jax.experimental import pallas as pl
from jax.experimental.pallas import tpu as pltpu
from jax.sharding import PartitionSpec as P

NORM_EPS = 1e-6
CORES = 2
BF16 = jnp.bfloat16
F32 = jnp.float32
MESH_ID = pl.DeviceIdType.MESH


def rms_norm(values, gain):
    wide = values.astype(jnp.float32)
    scaled = wide * lax.rsqrt(jnp.mean(wide * wide, axis=-1, keepdims=True) + NORM_EPS)
    return (scaled * gain.astype(jnp.float32)).astype(jnp.bfloat16)


def add_rows(first, second):
    return (first.astype(jnp.float32) + second.astype(jnp.float32)).astype(jnp.bfloat16)


def attn_out(x_rows, norm_gain, w_q, w_k, w_v, w_o):
    tokens = x_rows.shape[0]
    heads = w_q.shape[1]
    kv_heads = w_k.shape[1]
    head_dim = w_q.shape[2]
    normed = rms_norm(x_rows, norm_gain)
    query = jnp.einsum('td,dhe->the', normed, w_q, preferred_element_type=jnp.float32).astype(jnp.bfloat16)
    query = query.reshape(tokens, kv_heads, heads // kv_heads, head_dim)
    key_proj = jnp.einsum('td,dge->tge', normed, w_k, preferred_element_type=jnp.float32).astype(jnp.bfloat16)
    val_proj = jnp.einsum('td,dge->tge', normed, w_v, preferred_element_type=jnp.float32).astype(jnp.bfloat16)
    scores = jnp.einsum('tgre,mge->grtm', query, key_proj, preferred_element_type=jnp.float32) * head_dim ** -0.5
    causal = jnp.arange(tokens)[:, None] >= jnp.arange(tokens)[None, :]
    scores = jnp.where(causal, scores, -1e30)
    probs = jax.nn.softmax(scores, axis=-1).astype(jnp.bfloat16)
    context = jnp.einsum('grtm,mge->tgre', probs, val_proj, preferred_element_type=jnp.float32).astype(jnp.bfloat16)
    context = context.reshape(tokens, heads, head_dim)
    return jnp.einsum('the,hed->td', context, w_o, preferred_element_type=jnp.float32).astype(jnp.bfloat16)


def slot_tables(eid, slot, gate, experts):
    hit = eid[:, :, None] == jnp.arange(experts)[None, None, :]
    slots = jnp.sum(jnp.where(hit, slot[:, :, None] + 1, 0), axis=1) - 1
    gates = jnp.sum(jnp.where(hit, gate[:, :, None].astype(F32), 0.0), axis=1)
    return slots.astype(BF16), gates.astype(BF16)


def grid_of(group):
    side = int(round((group // CORES) ** 0.5))
    return side, group // CORES // side


def combine_kernel(side_y, side_x, o_ref, base_ref, meta_l, meta_r, out_ref, r1l, r1r, ps_l, ps_r, p2l, p2r, loc_sem, s1, v1, s2, v2):
    me = lax.axis_index('expert')
    core = me % CORES
    x = (me // CORES) % side_x
    y = me // (CORES * side_x)
    row_peers = side_x * CORES
    col_peers = side_y * CORES
    q_row = x * CORES + core
    q_col = y * CORES + core
    half = o_ref.shape[-1] // 2
    slots = o_ref.shape[-2]

    def dev(yy, xx, cc):
        return {'expert': (yy * side_x + xx) * CORES + cc}

    row_moves = [(dx, dc) for dx in range(side_x) for dc in range(CORES) if (dx, dc) != (0, 0)]
    col_moves = [(dy, dc) for dy in range(side_y) for dc in range(CORES) if (dy, dc) != (0, 0)]
    barrier = pltpu.get_barrier_semaphore()
    partners = [((y), (x + dx) % side_x, (core + dc) % CORES) for dx, dc in row_moves]
    partners += [((y + dy) % side_y, x, (core + dc) % CORES) for dy, dc in col_moves if dy]
    for spot in partners:
        pl.semaphore_signal(barrier, inc=1, device_id=dev(*spot), device_id_type=MESH_ID)
    pl.semaphore_wait(barrier, len(partners))

    def start_l(i, dx, dc):
        xt, ct = (x + dx) % side_x, (core + dc) % CORES
        copy = pltpu.make_async_remote_copy(src_ref=o_ref.at[:, xt, ct, :, pl.ds(0, half)], dst_ref=r1l.at[:, q_row], send_sem=s1.at[0, i], recv_sem=v1.at[0, i], device_id=dev(y, xt, ct), device_id_type=MESH_ID)
        copy.start()
        return copy

    def start_r(i, dy, dc):
        yt, ct = (y + dy) % side_y, (core + dc) % CORES
        copy = pltpu.make_async_remote_copy(src_ref=o_ref.at[yt, :, ct, :, pl.ds(half, half)], dst_ref=r1r.at[:, q_col], send_sem=s1.at[1, i], recv_sem=v1.at[1, i], device_id=dev(yt, x, ct), device_id_type=MESH_ID)
        copy.start()
        return copy

    first = []
    for i in range(max(len(row_moves), len(col_moves))):
        if i < len(row_moves):
            first.append(start_l(i, *row_moves[i]))
        if i < len(col_moves):
            first.append(start_r(i, *col_moves[i]))
    own_l = pltpu.make_async_copy(o_ref.at[:, x, core, :, pl.ds(0, half)], r1l.at[:, q_row], loc_sem.at[0])
    own_r = pltpu.make_async_copy(o_ref.at[y, :, core, :, pl.ds(half, half)], r1r.at[:, q_col], loc_sem.at[1])
    own_l.start()
    own_r.start()
    own_l.wait()
    own_r.wait()
    for copy in first:
        copy.wait()

    lane = lax.broadcasted_iota(jnp.int32, (1, slots), 1).astype(F32)

    def partial(meta, landed, sums, k, peers):
        table = meta[k].astype(F32)
        weights = []
        for q in range(peers):
            weights.append(jnp.where(table[:, q:q + 1] == lane, table[:, peers + q:peers + q + 1], 0.0).astype(BF16))
        weight = jnp.concatenate(weights, axis=1)
        vals = landed[k].reshape(peers * slots, half)
        sums[k] = jnp.dot(weight, vals, preferred_element_type=F32)

    def send_l(i):
        yt = (y + i) % side_y
        copy = pltpu.make_async_remote_copy(src_ref=ps_l.at[yt], dst_ref=p2l.at[i], send_sem=s2.at[0, i], recv_sem=v2.at[0, i], device_id=dev(yt, x, core), device_id_type=MESH_ID)
        copy.start()
        return copy

    def send_r(i):
        xt = (x + i) % side_x
        copy = pltpu.make_async_remote_copy(src_ref=ps_r.at[xt], dst_ref=p2r.at[i], send_sem=s2.at[1, i], recv_sem=v2.at[1, i], device_id=dev(y, xt, core), device_id_type=MESH_ID)
        copy.start()
        return copy

    second = []
    for i in range(1, max(side_y, side_x) + 1):
        if i < side_y:
            partial(meta_l, r1l, ps_l, (y + i) % side_y, row_peers)
        elif i == side_y:
            partial(meta_l, r1l, ps_l, y, row_peers)
        if 1 <= i - 1 < side_x:
            second.append(send_r(i - 1))
        if i < side_x:
            partial(meta_r, r1r, ps_r, (x + i) % side_x, col_peers)
        elif i == side_x:
            partial(meta_r, r1r, ps_r, x, col_peers)
        if i < side_y:
            second.append(send_l(i))
    for copy in second:
        copy.wait()
    total_l = base_ref[:, :half].astype(F32) + ps_l[y]
    for i in range(1, side_y):
        total_l = total_l + p2l[i]
    out_ref[:, :half] = total_l.astype(BF16)
    total_r = base_ref[:, half:].astype(F32) + ps_r[x]
    for i in range(1, side_x):
        total_r = total_r + p2r[i]
    out_ref[:, half:] = total_r.astype(BF16)


def combine(out_slots, base, meta_l, meta_r, group):
    side_y, side_x = grid_of(group)
    capacity = out_slots.shape[0] // group
    dim = out_slots.shape[-1]
    rows = base.shape[0]
    half = dim // 2
    cube = out_slots.reshape(side_y, side_x, CORES, capacity, dim)
    return pl.pallas_call(
        functools.partial(combine_kernel, side_y, side_x),
        out_shape=jax.ShapeDtypeStruct(base.shape, BF16),
        in_specs=[pl.BlockSpec(memory_space=pl.ANY)] + [pl.BlockSpec(memory_space=pltpu.VMEM)] * 3,
        out_specs=pl.BlockSpec(memory_space=pltpu.VMEM),
        scratch_shapes=[
            pltpu.VMEM((side_y, side_x * CORES, capacity, half), BF16),
            pltpu.VMEM((side_x, side_y * CORES, capacity, half), BF16),
            pltpu.VMEM((side_y, rows, half), F32),
            pltpu.VMEM((side_x, rows, half), F32),
            pltpu.VMEM((side_y, rows, half), F32),
            pltpu.VMEM((side_x, rows, half), F32),
            pltpu.SemaphoreType.DMA((2,)),
            pltpu.SemaphoreType.DMA((2, max(side_x, side_y) * CORES)),
            pltpu.SemaphoreType.DMA((2, max(side_x, side_y) * CORES)),
            pltpu.SemaphoreType.DMA((2, max(side_x, side_y))),
            pltpu.SemaphoreType.DMA((2, max(side_x, side_y))),
        ],
        compiler_params=pltpu.CompilerParams(collective_id=0, has_side_effects=True, vmem_limit_bytes=60000000),
    )(cube, base, meta_l, meta_r)


def combine_tables(slots, gates, group):
    side_y, side_x = grid_of(group)
    experts = slots.shape[-1]
    me = lax.axis_index('expert')
    core = me % CORES
    x = (me // CORES) % side_x
    y = me // (CORES * side_x)

    def cut(table):
        cube = table.reshape(side_y, side_x, CORES, -1, side_y, side_x, CORES)
        left = lax.dynamic_slice(cube, (0, x, core, 0, y, 0, 0), (side_y, 1, 1, cube.shape[3], 1, side_x, CORES))
        right = lax.dynamic_slice(cube, (y, 0, core, 0, 0, x, 0), (1, side_x, 1, cube.shape[3], side_y, 1, CORES))
        return left.reshape(side_y, -1, side_x * CORES), right.reshape(side_x, -1, side_y * CORES)
    sl, sr = cut(slots)
    gl, gr = cut(gates)
    return jnp.concatenate([sl, gl], axis=-1), jnp.concatenate([sr, gr], axis=-1)


def solution(mesh):
    group = mesh.shape['expert']

    def local_step(x_a, x_b, dy_b, eid_a, slot_a, gate_a, eid_b, slot_b, gate_b, u_b, norm_1, norm_2, w_q, w_k, w_v, w_o, w_1, w_2, w_3):
        experts = w_1.shape[0] * group
        capacity = u_b.shape[1] // group
        rows, model_dim = x_a.shape
        me = lax.axis_index('expert')
        w1, w2, w3 = w_1[0], w_2[0], w_3[0]

        tables = slot_tables(eid_a, slot_a, gate_a, experts) + slot_tables(eid_b, slot_b, gate_b, experts)
        meta = lax.all_gather(jnp.concatenate(tables, axis=1), 'expert', axis=0, tiled=True)
        dy_all = lax.all_gather(dy_b, 'expert', axis=0, tiled=True)
        slots_a, gates_a, slots_b, gates_b = [meta[:, i * experts:(i + 1) * experts] for i in range(4)]

        h_a = add_rows(x_a, attn_out(x_a, norm_1, w_q, w_k, w_v, w_o))
        u_a = rms_norm(h_a, norm_2)
        u_all = lax.all_gather(u_a, 'expert', axis=0, tiled=True)
        attn_val, attn_pull = jax.vjp(attn_out, x_b, norm_1, w_q, w_k, w_v, w_o)
        h_b = add_rows(x_b, attn_val)

        def mine(table):
            return lax.dynamic_slice_in_dim(table, me, 1, axis=1).reshape(group, 1, rows).astype(F32)

        place = jnp.arange(capacity, dtype=F32)[None, :, None]

        saved = u_b[0]
        pre_1 = jnp.dot(saved, w1, preferred_element_type=F32).astype(BF16).astype(F32)
        pre_3 = jnp.dot(saved, w3, preferred_element_type=F32).astype(BF16).astype(F32)
        sigma = jax.nn.sigmoid(pre_1)
        silu_1 = pre_1 * sigma
        hid_b = (silu_1 * pre_3).astype(BF16)
        pick_b = jnp.where(mine(slots_b) == place, mine(gates_b), 0.0).astype(BF16)
        d_out = jnp.einsum('pst,ptd->psd', pick_b, dy_all.reshape(group, rows, model_dim), preferred_element_type=F32).astype(BF16).reshape(group * capacity, model_dim)
        grad_hid = jnp.einsum('cd,fd->cf', d_out, w2, preferred_element_type=F32).astype(BF16).astype(F32)
        grad_a1 = (grad_hid * pre_3 * sigma * (1.0 + pre_1 * (1.0 - sigma))).astype(BF16)
        grad_a3 = (grad_hid * silu_1).astype(BF16)
        grad_in = (jnp.einsum('cf,df->cd', grad_a1, w1, preferred_element_type=F32) + jnp.einsum('cf,df->cd', grad_a3, w3, preferred_element_type=F32)).astype(BF16)
        ml, mr = combine_tables(slots_b, jnp.ones_like(gates_b), group)
        du = combine(grad_in, jnp.zeros_like(x_b), ml, mr, group)

        pick_a = (mine(slots_a) == place).astype(BF16)
        recv = jnp.einsum('pst,ptd->psd', pick_a, u_all.reshape(group, rows, model_dim), preferred_element_type=F32).astype(BF16).reshape(group * capacity, model_dim)
        act_1 = jnp.dot(recv, w1, preferred_element_type=F32).astype(BF16).astype(F32)
        act_3 = jnp.dot(recv, w3, preferred_element_type=F32).astype(BF16).astype(F32)
        hidden = (act_1 * jax.nn.sigmoid(act_1) * act_3).astype(BF16)
        out_a = jnp.dot(hidden, w2, preferred_element_type=F32).astype(BF16)
        ml, mr = combine_tables(slots_a, gates_a, group)
        y_a = combine(out_a, h_a, ml, mr, group)

        grad_w2 = jnp.einsum('cf,cd->fd', hid_b, d_out, preferred_element_type=F32)
        grad_w1 = jnp.einsum('cd,cf->df', saved, grad_a1, preferred_element_type=F32)
        grad_w3 = jnp.einsum('cd,cf->df', saved, grad_a3, preferred_element_type=F32)

        _, norm_pull = jax.vjp(rms_norm, h_b, norm_2)
        dh_norm, g_n2 = norm_pull(du)
        dh = add_rows(dy_b, dh_norm)
        grad_x, g_n1, g_q, g_k, g_v, g_o = attn_pull(dh)
        dx_b = add_rows(dh, grad_x)
        grads = [g.astype(F32)[None] for g in (g_q, g_k, g_v, g_o, g_n1, g_n2)]
        return (y_a, dx_b, grad_w1[None], grad_w2[None], grad_w3[None], *grads)

    row_spec = P(('data', 'expert'), None)
    cube_spec = P(('data', 'expert'), None, None)
    quad_spec = P(('data', 'expert'), None, None, None)
    expert_spec = P('expert', None, None)
    in_specs = (row_spec, row_spec, row_spec, row_spec, row_spec, row_spec, row_spec, row_spec, row_spec, cube_spec, P(), P(), P(), P(), P(), P(), expert_spec, expert_spec, expert_spec)
    out_specs = (row_spec, row_spec, cube_spec, cube_spec, cube_spec, quad_spec, quad_spec, quad_spec, quad_spec, row_spec, row_spec)
    return jax.shard_map(local_step, mesh=mesh, in_specs=in_specs, out_specs=out_specs, check_vma=False)
```

time: 679 us -> 480 us (0.71)
  the two profiles are of different devices: /device:TPU:103 before, /device:TPU:97 now
where the time goes in v1:
time: 480 us; the launch traced here: 470 us
  matrix products  166 us (35%)
  Pallas kernels  159 us (33%)
  waiting for transfers between devices  55.5 us (12%)
  local copies, waits for them, and re-layouts  39.4 us (8%)
  other arithmetic  34.7 us (7%)
  between operations  14.8 us (3%)
    pallas_call x2, Pallas kernels, combine(): pl.pallas_call(functools.partial(combine_kernel, side_y, side_x), out_sha...  159 us
    all_gather x1, waiting for transfers between devices, local_step(): dy_all = lax.all_gather(dy_b, 'expert', axis=0, tiled=True)  51.8 us
    unnamed x105, local copies, waits for them, and re-layouts  16 us
    dot_general x1, matrix products, local_step(): out_a = jnp.dot(hidden, w2, preferred_element_type=F32).astype(BF16)  15.4 us
    dot_general x1, matrix products, local_step(): jnp.dot(saved, w3, preferred_element_type=F32).astype(BF16).astype(F32)  13.8 us
    dot_general x1, matrix products, local_step(): jnp.einsum('cf,df->cd', grad_a3, w3, preferred_element_type=F32)  13.2 us
    dot_general x1, matrix products, local_step(): jnp.einsum('cd,cf->df', saved, grad_a3, preferred_element_type=F32)  11.9 us
    dot_general x1, matrix products, local_step(): jnp.einsum('pst,ptd->psd', pick_b, dy_all.reshape(group, rows, model_dim)...  11.4 us
  transfers between devices with their start and end apart: 3, of which 2 were waited for; matrix products, arithmetic and copies ran while one was open for 28% of the time, Pallas kernels for 0%

profile of v1, /device:TPU:97, one launch (start us, length us, event | category | flops | bytes accessed | tf_op | source)
XLA Modules:
  0.0 470.4 jit_solution(15757492027864442602)
XLA Ops:
  21.4 2.8 fusion.139
  34.0 4.7 fusion.160
  38.7 3.0 fusion.60
  44.8 10.0 %fusion.26 = bf16[4096,512]{1,0:T(8,128)(2,1)} fusion(bf16[1,4096,1024]{2,1,0:T(8,128)(2,1)} %param.28, bf16[1,1024,512]{2,1,0:T(8,128)(2,1)S(1)} %copy-done.39), kind=kOutput, calls=%fused_computation.36 | convolution fusion | flops 4297064448 | bytes 13631488 | tf_op jit(solution)/shard_map/dot_general | solution.py:232
  54.7 2.9 all-gather.4.cloned.1.call-done
  57.6 2.9 fusion.159
  74.5 51.8 %all-gather.8.cloned.1.call-done = bf16[8192,1024]{1,0:T(8,128)(2,1)} async-done(((bf16[256,1024]{1,0:T(8,128)(2,1)}), bf16[8192,1024]{1,0:T(8,128)(2,1)}) %all-gather.8.cloned.1.call-update) | async-done | bytes 16777232 | tf_op jit(solution)/shard_map/all_gather | solution.py:217
  126.3 11.4 %convolution_convert_fusion.1 = bf16[32,128,1024]{2,1,0:T(8,128)(2,1)} fusion(bf16[32,256,1024]{2,1,0:T(8,128)(2,1)} %bitcast.298, bf16[32,256]{1,0:T(8,128)(2,1)S(1)} %reshape.240, f32[32,256]{1,0:T(8,128)S(1)} %reshape.239), kind=kOutput, calls=%fused_computation.33 | convolution fusion | flops 2153775104 | bytes 25214976 | tf_op jit(solution)/shard_map/pst,ptd->psd/dot_general | solution.py:238
  137.8 8.3 %convolution_convert_fusion.3 = bf16[4096,512]{1,0:T(8,128)(2,1)S(1)} fusion(bf16[4096,1024]{1,0:T(8,128)(2,1)} %bitcast.302, bf16[1,512,1024]{2,1,0:T(8,128)(2,1)S(1)} %copy-done.37), kind=kOutput, calls=%fused_computation.37 | convolution fusion | flops 4297064448 | bytes 13631488 | tf_op jit(solution)/shard_map/cd,fd->cf/dot_general | solution.py:239
  146.2 13.8 %fusion.8 = (bf16[4096,512]{1,0:T(8,128)(2,1)S(1)}, bf16[4096,512]{1,0:T(8,128)(2,1)}) fusion(bf16[4096,512]{1,0:T(8,128)(2,1)S(1)} %convolution_convert_fusion.3, bf16[4096,512]{1,0:T(8,128)(2,1)S(1)} %copy-done.42, bf16[1,1024,512]{2,1,0:T(8,128)(2,1)S(1)} %copy-done.35, bf16[1,4096,1024]{2,1,0:T(8,128)(2,1)} %param.28), kind=kOutput, calls=%fused_computation.17 | convolution fusion | flops 4324327424 | bytes 26214400 | tf_op jit(solution)/shard_map/dot_general | solution.py:233
  160.0 8.4 %fusion.97 = f32[4096,1024]{1,0:T(8,128)} fusion(bf16[4096,512]{1,0:T(8,128)(2,1)S(1)} %get-tuple-element.67, bf16[1,1024,512]{2,1,0:T(8,128)(2,1)S(1)} %copy-done.40), kind=kOutput, calls=%fused_computation.146 | convolution fusion | flops 4294967296 | bytes 22020096 | tf_op jit(solution)/shard_map/cf,df->cd/dot_general | solution.py:242
  168.4 13.2 %add_convert_fusion = bf16[4096,1024]{1,0:T(8,128)(2,1)} fusion(f32[4096,1024]{1,0:T(8,128)} %fusion.97, bf16[1,1024,512]{2,1,0:T(8,128)(2,1)S(1)} %copy-done.35, bf16[4096,512]{1,0:T(8,128)(2,1)} %copy-done.44, bf16[4096,512]{1,0:T(8,128)(2,1)} %fusion.26), kind=kOutput, calls=%fused_computation.1 | convolution fusion | flops 4320133120 | bytes 34603008 | tf_op jit(solution)/shard_map/cf,df->cd/dot_general | solution.py:242
  182.6 79.7 %shard_map.267 = bf16[256,1024]{1,0:T(8,128)(2,1)} custom-call(bf16[4,4,2,128,1024]{4,3,2,1,0:T(8,128)(2,1)} %bitcast.306, bf16[256,1024]{1,0:T(8,128)(2,1)} %broadcast_in_dim.157.base_ref, bf16[4,256,16]{2,1,0:T(8,128)(2,1)} %concatenate.18.meta_l, bf16[4,256,16]{2,1,0:T(8,128)(2,1)} %concatenate.19.meta_r), custom_call_target="tpu_custom_call" | custom-call | tf_op jit(solution)/shard_map/pallas_call | solution.py:165
  283.2 11.9 %fusion.57 = f32[1,1024,512]{1,2,0:T(8,128)} fusion(bf16[1,4096,1024]{2,1,0:T(8,128)(2,1)} %param.28, bf16[4096,512]{1,0:T(8,128)(2,1)} %copy-done.44, bf16[4096,512]{1,0:T(8,128)(2,1)} %fusion.26), kind=kOutput, calls=%fused_computation.85 | convolution fusion | flops 4311744512 | bytes 18874368 | tf_op jit(solution)/shard_map/cd,cf->df/dot_general | solution.py:257
  295.0 2.9 copy.90
  297.9 10.5 %fusion.54 = f32[1,1024,512]{1,2,0:T(8,128)} fusion(bf16[4096,512]{1,0:T(8,128)(2,1)} %copy-done.41, bf16[1,4096,1024]{2,1,0:T(8,128)(2,1)} %param.28), kind=kOutput, calls=%fused_computation.84 | convolution fusion | flops 4294967296 | bytes 14680064 | tf_op jit(solution)/shard_map/cd,cf->df/dot_general | solution.py:256
  308.4 3.3 copy.89
  314.7 3.9 fusion.36
  330.3 2.8 bitcast_convert_fusion
  339.3 6.3 %fusion.51 = f32[1,512,1024]{2,1,0:T(8,128)} fusion(bf16[4096,1024]{1,0:T(8,128)(2,1)S(1)} %bitcast.305, bf16[4096,512]{1,0:T(8,128)(2,1)S(1)} %copy-done.45, bf16[4096,512]{1,0:T(8,128)(2,1)S(1)} %copy-done.43), kind=kOutput, calls=%fused_computation.83 | convolution fusion | flops 4311744512 | bytes 18874368 | tf_op jit(solution)/shard_map/cf,cd->fd/dot_general | solution.py:255
  345.6 11.4 %convolution_convert_fusion.2 = bf16[32,128,1024]{2,1,0:T(8,128)(2,1)} fusion(bf16[32,256,1024]{2,1,0:T(8,128)(2,1)} %bitcast.297, f32[32,256]{1,0:T(8,128)S(1)} %reshape.238), kind=kOutput, calls=%fused_computation.34 | convolution fusion | flops 2152726528 | bytes 25198592 | tf_op jit(solution)/shard_map/pst,ptd->psd/dot_general | solution.py:247
  357.1 9.5 %convolution_convert_fusion.4 = bf16[4096,512]{1,0:T(8,128)(2,1)} fusion(bf16[4096,1024]{1,0:T(8,128)(2,1)} %bitcast.300, bf16[1,1024,512]{2,1,0:T(8,128)(2,1)S(1)} %copy-done.36), kind=kOutput, calls=%fused_computation.38 | convolution fusion | flops 4297064448 | bytes 13631488 | tf_op jit(solution)/shard_map/dot_general | solution.py:249
  366.6 15.4 %convolution_convert_fusion = bf16[4096,1024]{1,0:T(8,128)(2,1)} fusion(bf16[4096,512]{1,0:T(8,128)(2,1)} %convolution_convert_fusion.4, bf16[4096,1024]{1,0:T(8,128)(2,1)} %bitcast.301, bf16[1,512,1024]{2,1,0:T(8,128)(2,1)S(1)} %copy-done.38, bf16[1,1024,512]{2,1,0:T(8,128)(2,1)} %param.35), kind=kOutput, calls=%fused_computation.32 | convolution fusion | flops 8613003264 | bytes 23068672 | tf_op jit(solution)/shard_map/dot_general | solution.py:251
  382.0 79.7 %shard_map.266 = bf16[256,1024]{1,0:T(8,128)(2,1)} custom-call(bf16[4,4,2,128,1024]{4,3,2,1,0:T(8,128)(2,1)} %bitcast.307, bf16[256,1024]{1,0:T(8,128)(2,1)} %get-tuple-element.74.base_ref, bf16[4,256,16]{2,1,0:T(8,128)(2,1)} %pad_maximum_fusion.meta_l, bf16[4,256,16]{2,1,0:T(8,128)(2,1)} %pad_maximum_fusion.1.meta_r), custom_call_target="tpu_custom_call" | custom-call | tf_op jit(solution)/shard_map/pallas_call | solution.py:165
  (188 shorter events, 85.0 us)
Async XLA Ops:
  7.2 18.9 %copy-start = (bf16[1024,16,64]{0,2,1:T(8,128)(2,1)S(1)}, bf16[1024,16,64]{0,2,1:T(8,128)(2,1)}, u32[]{:S(2)}) copy-start(bf16[1024,16,64]{0,2,1:T(8,128)(2,1)} %param.31) | copy-start | bytes 6291460
  7.2 14.2 %copy-start.12 = (bf16[256,1024]{1,0:T(8,128)(2,1)S(1)}, bf16[256,1024]{1,0:T(8,128)(2,1)}, u32[]{:S(2)}) copy-start(bf16[256,1024]{1,0:T(8,128)(2,1)} %param.19) | copy-start | bytes 1572868
  7.2 50.4 %all-gather.4.cloned.1.call-start = ((), (), s32[]{:S(2)}) async-start(), calls=%async_computation | async-start | bytes 2162688 | tf_op jit(solution)/shard_map/all_gather | solution.py:216
  13.9 11.6 %copy-start.5 = (bf16[256,1024]{1,0:T(8,128)(2,1)S(1)}, bf16[256,1024]{1,0:T(8,128)(2,1)}, u32[]{:S(2)}) copy-start(bf16[256,1024]{1,0:T(8,128)(2,1)} %param.20) | copy-start | bytes 1572868
  13.9 112.4 %all-gather.8.cloned.1.call-start = ((), (), s32[]{:S(2)}) async-start(), calls=%async_computation.2 | async-start | bytes 17301504 | tf_op jit(solution)/shard_map/all_gather | solution.py:217
  14.7 330.9 %all-gather.6.cloned.1.call-start = ((), (), s32[]{:S(2)}) async-start(), calls=%async_computation.1 | async-start | bytes 17301504 | tf_op jit(solution)/shard_map/all_gather | solution.py:222
  15.5 16.9 %copy-start.19 = (f32[1024]{0:T(1024)}, f32[1024]{0:T(1024)S(1)}, u32[]{:S(2)}) copy-start(f32[1024]{0:T(1024)S(1)} %convert_element_type.348) | copy-start | bytes 12292
  16.8 7.3 %copy-start.32 = (bf16[1024,8,64]{0,2,1:T(8,128)(2,1)S(1)}, bf16[1024,8,64]{0,2,1:T(8,128)(2,1)}, u32[]{:S(2)}) copy-start(bf16[1024,8,64]{0,2,1:T(8,128)(2,1)} %param.33) | copy-start | bytes 3145732
  44.1 10.6 %copy-start.28 = (f32[256]{0:T(256)}, f32[256]{0:T(256)S(1)}, u32[]{:S(2)}) copy-start(f32[256]{0:T(256)S(1)} %get-tuple-element.69) | copy-start | bytes 3076
  44.1 218.2 %copy-start.8 = (bf16[256,1024]{1,0:T(8,128)(2,1)}, bf16[256,1024]{1,0:T(8,128)(2,1)S(1)}, u32[]{:S(2)}) copy-start(bf16[256,1024]{1,0:T(8,128)(2,1)S(1)} %get-tuple-element.70) | copy-start | bytes 1572868
  126.3 11.4 %copy-start.37 = (bf16[1,512,1024]{2,1,0:T(8,128)(2,1)S(1)}, bf16[1,512,1024]{2,1,0:T(8,128)(2,1)}, u32[]{:S(2)}) copy-start(bf16[1,512,1024]{2,1,0:T(8,128)(2,1)} %param.36) | copy-start | bytes 3145732
  137.8 8.3 %copy-start.35 = (bf16[1,1024,512]{2,1,0:T(8,128)(2,1)S(1)}, bf16[1,1024,512]{2,1,0:T(8,128)(2,1)}, u32[]{:S(2)}) copy-start(bf16[1,1024,512]{2,1,0:T(8,128)(2,1)} %param.37) | copy-start | bytes 3145732
  137.8 8.4 %copy-start.42 = (bf16[4096,512]{1,0:T(8,128)(2,1)S(1)}, bf16[4096,512]{1,0:T(8,128)(2,1)}, u32[]{:S(2)}) copy-start(bf16[4096,512]{1,0:T(8,128)(2,1)} %fusion.26) | copy-start | bytes 12582916
  146.1 13.8 %copy-start.44 = (bf16[4096,512]{1,0:T(8,128)(2,1)}, bf16[4096,512]{1,0:T(8,128)(2,1)S(1)}, u32[]{:S(2)}) copy-start(bf16[4096,512]{1,0:T(8,128)(2,1)S(1)} %convolution_convert_fusion.3) | copy-start | bytes 12582916
  146.2 13.8 %copy-start.40 = (bf16[1,1024,512]{2,1,0:T(8,128)(2,1)S(1)}, bf16[1,1024,512]{2,1,0:T(8,128)(2,1)}, u32[]{:S(2)}) copy-start(bf16[1,1024,512]{2,1,0:T(8,128)(2,1)} %param.35) | copy-start | bytes 3145732
  160.0 8.4 %copy-start.41 = (bf16[4096,512]{1,0:T(8,128)(2,1)}, bf16[4096,512]{1,0:T(8,128)(2,1)S(1)}, u32[]{:S(2)}) copy-start(bf16[4096,512]{1,0:T(8,128)(2,1)S(1)} %get-tuple-element.67) | copy-start | bytes 12582916
  182.6 79.8 %copy-start.21 = (f32[1024]{0:T(1024)S(1)}, f32[1024]{0:T(1024)}, u32[]{:S(2)}) copy-start(f32[1024]{0:T(1024)} %convert_element_type.360) | copy-start | bytes 12292
  182.6 79.8 %copy-start.25 = (f32[256]{0:T(256)S(1)}, f32[256]{0:T(256)}, u32[]{:S(2)}) copy-start(f32[256]{0:T(256)} %get-tuple-element.85) | copy-start | bytes 3076
  182.6 81.9 %copy-start.29 = (f32[256]{0:T(256)S(1)}, f32[256]{0:T(256)}, u32[]{:S(2)}) copy-start(f32[256]{0:T(256)} %copy-done.28) | copy-start | bytes 3076
  182.6 81.9 %copy-start.7 = (bf16[256,1024]{1,0:T(8,128)(2,1)S(1)}, bf16[256,1024]{1,0:T(8,128)(2,1)}, u32[]{:S(2)}) copy-start(bf16[256,1024]{1,0:T(8,128)(2,1)} %get-tuple-element.74.base_ref) | copy-start | bytes 1572868
  182.6 81.9 %copy-start.11 = (bf16[256,1024]{1,0:T(8,128)(2,1)S(1)}, bf16[256,1024]{1,0:T(8,128)(2,1)}, u32[]{:S(2)}) copy-start(bf16[256,1024]{1,0:T(8,128)(2,1)} %param.21) | copy-start | bytes 1572868
  182.6 81.9 %copy-start.31 = (f32[256]{0:T(256)S(1)}, f32[256]{0:T(256)}, u32[]{:S(2)}) copy-start(f32[256]{0:T(256)} %get-tuple-element.84) | copy-start | bytes 3076
  345.6 11.4 %copy-start.36 = (bf16[1,1024,512]{2,1,0:T(8,128)(2,1)S(1)}, bf16[1,1024,512]{2,1,0:T(8,128)(2,1)}, u32[]{:S(2)}) copy-start(bf16[1,1024,512]{2,1,0:T(8,128)(2,1)} %param.37) | copy-start | bytes 3145732
  357.1 9.5 %copy-start.38 = (bf16[1,512,1024]{2,1,0:T(8,128)(2,1)S(1)}, bf16[1,512,1024]{2,1,0:T(8,128)(2,1)}, u32[]{:S(2)}) copy-start(bf16[1,512,1024]{2,1,0:T(8,128)(2,1)} %param.36) | copy-start | bytes 3145732
  (27 other events, 86.7 us)
Sparse Core Ops, SparseCore 0:
  14.0 43.5 all-gather.3
  59.7 66.5 all-gather.7
  267.2 66.9 all-gather.5

commit v2 on v0

v2 whole, which is shorter than its diff:
```python
import functools

import jax
import jax.numpy as jnp
from jax import lax
from jax.experimental import pallas as pl
from jax.experimental.pallas import tpu as pltpu
from jax.sharding import PartitionSpec as P

NORM_EPS = 1e-6
CORES = 2
BF16 = jnp.bfloat16
F32 = jnp.float32
MESH_ID = pl.DeviceIdType.MESH


def rms_norm(values, gain):
    wide = values.astype(jnp.float32)
    scaled = wide * lax.rsqrt(jnp.mean(wide * wide, axis=-1, keepdims=True) + NORM_EPS)
    return (scaled * gain.astype(jnp.float32)).astype(jnp.bfloat16)


def add_rows(first, second):
    return (first.astype(jnp.float32) + second.astype(jnp.float32)).astype(jnp.bfloat16)


def attn_out(x_rows, norm_gain, w_q, w_k, w_v, w_o):
    tokens = x_rows.shape[0]
    heads = w_q.shape[1]
    kv_heads = w_k.shape[1]
    head_dim = w_q.shape[2]
    normed = rms_norm(x_rows, norm_gain)
    query = jnp.einsum('td,dhe->the', normed, w_q, preferred_element_type=jnp.float32).astype(jnp.bfloat16)
    query = query.reshape(tokens, kv_heads, heads // kv_heads, head_dim)
    key_proj = jnp.einsum('td,dge->tge', normed, w_k, preferred_element_type=jnp.float32).astype(jnp.bfloat16)
    val_proj = jnp.einsum('td,dge->tge', normed, w_v, preferred_element_type=jnp.float32).astype(jnp.bfloat16)
    scores = jnp.einsum('tgre,mge->grtm', query, key_proj, preferred_element_type=jnp.float32) * head_dim ** -0.5
    causal = jnp.arange(tokens)[:, None] >= jnp.arange(tokens)[None, :]
    scores = jnp.where(causal, scores, -1e30)
    probs = jax.nn.softmax(scores, axis=-1).astype(jnp.bfloat16)
    context = jnp.einsum('grtm,mge->tgre', probs, val_proj, preferred_element_type=jnp.float32).astype(jnp.bfloat16)
    context = context.reshape(tokens, heads, head_dim)
    return jnp.einsum('the,hed->td', context, w_o, preferred_element_type=jnp.float32).astype(jnp.bfloat16)


def slot_tables(eid, slot, gate, experts):
    hit = eid[:, :, None] == jnp.arange(experts)[None, None, :]
    slots = jnp.sum(jnp.where(hit, slot[:, :, None] + 1, 0), axis=1) - 1
    gates = jnp.sum(jnp.where(hit, gate[:, :, None].astype(F32), 0.0), axis=1)
    return slots.astype(BF16), gates.astype(BF16)


def place_of(side_x):
    me = lax.axis_index('expert')
    core = me % CORES
    return me, me // (CORES * side_x), (me // CORES) % side_x, core


def dev(side_x, yy, xx, cc):
    return {'expert': (yy * side_x + xx) * CORES + cc}


def greet(partners):
    barrier = pltpu.get_barrier_semaphore()
    for spot in partners:
        pl.semaphore_signal(barrier, inc=1, device_id=spot, device_id_type=MESH_ID)
    pl.semaphore_wait(barrier, len(partners))


class Gather:
    def __init__(self, side, buf, cut, send, recv):
        self.side, self.buf, self.send, self.recv = side, buf, send, recv
        _, self.y, self.x, self.core = place_of(side)
        width = buf.shape[-1]
        self.left, self.right = pl.ds(0, cut), pl.ds(cut, width - cut)
        self.count = 0
        y, x, c, side = self.y, self.x, self.core, self.side
        up, down, far = (y + 1) % side, (y + side - 1) % side, (y + 2) % side
        east, west, over = (x + 1) % side, (x + side - 1) % side, (x + 2) % side
        pair = side // 2
        lo, hi, every = pl.ds(0, pair), pl.ds(pair, pair), pl.ds(0, side)
        twin = 1 - c
        L, R = self.left, self.right
        self.own = []
        for k in (1, side - 1, 2):
            self.own.append(self.make((y, x, c, L), (y, (x + k) % side, c)))
            self.own.append(self.make((y, x, c, R), ((y + k) % side, x, c)))
        self.line = [self.make((y, every, c, L), (up, x, c)), self.make((every, x, c, R), (y, east, c)),
                     self.make((y, every, c, L), (down, x, c)), self.make((every, x, c, R), (y, west, c))]
        self.relay = [self.make((down, lo, c, L), (up, x, c)), self.make((lo, west, c, R), (y, east, c)),
                      self.make((up, hi, c, L), (down, x, c)), self.make((hi, east, c, R), (y, west, c))]
        self.twin_own = [self.make((y, every, c, L), (y, x, twin)), self.make((every, x, c, R), (y, x, twin))]
        self.twin_line = [self.make((up, every, c, L), (y, x, twin)), self.make((every, east, c, R), (y, x, twin)),
                          self.make((down, every, c, L), (y, x, twin)), self.make((every, west, c, R), (y, x, twin))]
        self.twin_far = [self.make((far, every, c, L), (y, x, twin)), self.make((every, over, c, R), (y, x, twin))]

    def make(self, spot, target):
        yy, xx, cc, cols = spot
        part = self.buf.at[yy, xx, cc, :, cols]
        i = self.count
        self.count += 1
        return pltpu.make_async_remote_copy(src_ref=part, dst_ref=part, send_sem=self.send.at[i], recv_sem=self.recv.at[i], device_id=dev(self.side, *target), device_id_type=MESH_ID)


GATHER_COPIES = 22


def start(copies):
    for copy in copies:
        copy.start()


def arrive(copies):
    for copy in copies:
        copy.wait_recv()


def sent(copies):
    for copy in copies:
        copy.wait_send()


def my_rows(table, experts, me, offset):
    row = lax.broadcasted_iota(jnp.int32, (8, table.shape[-1]), 0)
    lane = lax.broadcasted_iota(jnp.int32, (8, table.shape[-1]), 1)
    pick = ((lane == offset + me) & (row == 0)) | ((lane == offset + experts + me) & (row == 1))
    return lax.dot_general(jnp.where(pick, 1.0, 0.0).astype(BF16), table, (((1,), (1,)), ((), ())), preferred_element_type=F32)


BLOCKS = 4


def backward_kernel(side, experts, dy_ref, u_ref, ub_ref, w13_ref, w2_ref, u_all, meta_all, du_ref, gw1, gw2, gw3, buf, w13t, w2t, tile, dout, acts, dtile, loc, tin, tout, sa, ra, sb, rb):
    me, y, x, core = place_of(side)
    partners = [dev(side, y, (x + k) % side, core) for k in range(1, side)]
    partners += [dev(side, (y + k) % side, x, core) for k in range(1, side)]
    partners += [dev(side, y, x, 1 - core)]
    greet(partners)
    dim = u_ref.shape[-1]
    width = w2_ref.shape[0]
    own_dy = pltpu.make_async_copy(dy_ref, buf.at[y, x, core], loc.at[0])
    own_u = pltpu.make_async_copy(u_ref, u_all.at[y, x, core], loc.at[1])
    own_dy.start()
    own_u.start()
    first = Gather(side, buf, dim // 2, sa, ra)
    second = Gather(side, u_all, dim // 2 + dim // 8, sb, rb)
    own_dy.wait()
    start(first.own)
    w13t[...] = w13_ref[...].T
    w2t[...] = w2_ref[...].T
    gw1[...] = jnp.zeros_like(gw1)
    gw2[...] = jnp.zeros_like(gw2)
    gw3[...] = jnp.zeros_like(gw3)
    own_u.wait()
    arrive(first.own)
    start(first.line)
    start(first.twin_own)
    arrive(first.line)
    start(first.relay)
    start(first.twin_line)
    start(second.own)
    arrive(first.relay)
    start(first.twin_far)
    arrive(first.twin_own + first.twin_line + first.twin_far)

    slots = du_ref.shape[1]
    group = du_ref.shape[0]
    rows = BLOCKS * slots
    steps = group // BLOCKS

    def fetch(g, slot):
        return pltpu.make_async_copy(ub_ref.at[pl.ds(g * rows, rows)], tile.at[slot], tin.at[slot])

    def put(g, slot):
        return pltpu.make_async_copy(dtile.at[slot], du_ref.at[pl.ds(g * BLOCKS, BLOCKS)], tout.at[slot])

    fetch(0, 0).start()
    spot = lax.broadcasted_iota(jnp.int32, (slots, 1), 0).astype(F32)

    def step(g, carry):
        slot = g % 2
        fetch(g, slot).wait()

        @pl.when(g + 1 < steps)
        def _():
            fetch(g + 1, 1 - slot).start()
        for j in range(BLOCKS):
            p = g * BLOCKS + j
            block = buf.at[p // (side * CORES), (p // CORES) % side, p % CORES]
            lines = my_rows(block[:, dim:], experts, me, 2 * experts)
            pick = jnp.where(lines[0:1] == spot, lines[1:2], 0.0).astype(BF16)
            dout[pl.ds(j * slots, slots), :] = jnp.dot(pick, block[:, :dim], preferred_element_type=F32).astype(BF16)
        pre = jnp.dot(tile[slot], w13_ref[...], preferred_element_type=F32).astype(BF16).astype(F32)
        pre_1, pre_3 = pre[:, :width], pre[:, width:]
        sigma = jax.nn.sigmoid(pre_1)
        silu_1 = pre_1 * sigma
        hid = (silu_1 * pre_3).astype(BF16)
        grad_hid = jnp.dot(dout[...], w2t[...], preferred_element_type=F32).astype(BF16).astype(F32)
        acts[:, :width] = (grad_hid * pre_3 * sigma * (1.0 + pre_1 * (1.0 - sigma))).astype(BF16)
        acts[:, width:] = (grad_hid * silu_1).astype(BF16)

        @pl.when(g >= 2)
        def _():
            put(g - 2, slot).wait()
        grad_in = jnp.dot(acts[...], w13t[...], preferred_element_type=F32).astype(BF16)
        dtile[slot] = grad_in.reshape(BLOCKS, slots, dim)
        put(g, slot).start()
        over = (((0,), (0,)), ((), ()))
        gw2[...] += lax.dot_general(hid, dout[...], over, preferred_element_type=F32)
        both = lax.dot_general(tile[slot], acts[...], over, preferred_element_type=F32)
        gw1[...] += both[:, :width]
        gw3[...] += both[:, width:]

        @pl.when(g == 1)
        def _():
            arrive(second.own)
            start(second.line)
            start(second.twin_own)

        @pl.when(g == 6)
        def _():
            arrive(second.line)
            start(second.relay)
            start(second.twin_line)
        return carry

    lax.fori_loop(0, steps, step, 0)
    meta_out = pltpu.make_async_copy(buf.at[:, :, :, :, pl.ds(dim, buf.shape[-1] - dim)], meta_all, loc.at[0])
    meta_out.start()
    put(steps - 2, steps % 2).wait()
    put(steps - 1, 1 - steps % 2).wait()
    arrive(second.relay)
    start(second.twin_far)
    arrive(second.twin_own + second.twin_line + second.twin_far)
    for gather in (first, second):
        sent(gather.own + gather.line + gather.relay + gather.twin_own + gather.twin_line + gather.twin_far)
    meta_out.wait()


def run_backward(dy_ext, u_a, saved, w13, w2, group):
    side = int(round((group // CORES) ** 0.5))
    rows, dim = u_a.shape
    wide = dy_ext.shape[1]
    slots = saved.shape[0] // group
    width = w2.shape[0]
    tall = BLOCKS * slots
    any_spec, vmem = pl.BlockSpec(memory_space=pl.ANY), pl.BlockSpec(memory_space=pltpu.VMEM)
    return pl.pallas_call(
        functools.partial(backward_kernel, side, group),
        out_shape=[
            jax.ShapeDtypeStruct((side, side, CORES, rows, dim), BF16),
            jax.ShapeDtypeStruct((side, side, CORES, rows, wide - dim), BF16),
            jax.ShapeDtypeStruct((group, slots, dim), BF16),
            jax.ShapeDtypeStruct((dim, width), F32),
            jax.ShapeDtypeStruct((width, dim), F32),
            jax.ShapeDtypeStruct((dim, width), F32),
        ],
        in_specs=[any_spec, vmem, any_spec, vmem, vmem],
        out_specs=[any_spec, any_spec, any_spec, vmem, vmem, vmem],
        scratch_shapes=[
            pltpu.VMEM((side, side, CORES, rows, wide), BF16),
            pltpu.VMEM((2 * width, dim), BF16),
            pltpu.VMEM((dim, width), BF16),
            pltpu.VMEM((2, tall, dim), BF16),
            pltpu.VMEM((tall, dim), BF16),
            pltpu.VMEM((tall, 2 * width), BF16),
            pltpu.VMEM((2, BLOCKS, slots, dim), BF16),
            pltpu.SemaphoreType.DMA((2,)),
            pltpu.SemaphoreType.DMA((2,)),
            pltpu.SemaphoreType.DMA((2,)),
        ] + [pltpu.SemaphoreType.DMA((GATHER_COPIES,))] * 4,
        compiler_params=pltpu.CompilerParams(collective_id=0, has_side_effects=True, vmem_limit_bytes=64000000),
    )(dy_ext, u_a, saved, w13, w2)


def combine_kernel(side, experts, offset, gated, forward, *refs):
    if forward:
        o_ref, base_ref, meta_ref, u_all, w13_ref, w2_ref, out_ref, fwd_ref, meta, r1l, r1r, ps_l, ps_r, p2l, p2r, loc_sem, s1, v1, s2, v2, utile, recv, otile, tin, tout = refs
    else:
        o_ref, base_ref, meta_ref, out_ref, meta, r1l, r1r, ps_l, ps_r, p2l, p2r, loc_sem, s1, v1, s2, v2 = refs
    me, y, x, core = place_of(side)
    peers = side * CORES
    q_row = x * CORES + core
    q_col = y * CORES + core
    half = o_ref.shape[-1] // 2
    slots = o_ref.shape[-2]
    moves = [(k, dc) for k in range(1, side) for dc in range(CORES)] + [(0, 1)]
    partners = [(y, (x + k) % side, (core + dc) % CORES) for k, dc in moves]
    partners += [((y + k) % side, x, (core + dc) % CORES) for k, dc in moves if k]
    greet([dev(side, *spot) for spot in partners])

    first = []
    for i, (k, dc) in enumerate(moves):
        xt, yt, ct = (x + k) % side, (y + k) % side, (core + dc) % CORES
        first.append(pltpu.make_async_remote_copy(src_ref=o_ref.at[:, xt, ct, :, pl.ds(0, half)], dst_ref=r1l.at[:, q_row], send_sem=s1.at[0, i], recv_sem=v1.at[0, i], device_id=dev(side, y, xt, ct), device_id_type=MESH_ID))
        first.append(pltpu.make_async_remote_copy(src_ref=o_ref.at[yt, :, ct, :, pl.ds(half, half)], dst_ref=r1r.at[:, q_col], send_sem=s1.at[1, i], recv_sem=v1.at[1, i], device_id=dev(side, yt, x, ct), device_id_type=MESH_ID))
    start(first)
    own_l = pltpu.make_async_copy(o_ref.at[:, x, core, :, pl.ds(0, half)], r1l.at[:, q_row], loc_sem.at[0])
    own_r = pltpu.make_async_copy(o_ref.at[y, :, core, :, pl.ds(half, half)], r1r.at[:, q_col], loc_sem.at[1])
    meta_in = pltpu.make_async_copy(meta_ref, meta, loc_sem.at[2])
    own_l.start()
    own_r.start()
    meta_in.start()
    meta_in.wait()

    if forward:
        width = w2_ref.shape[0]
        group = fwd_ref.shape[0]
        steps = group // BLOCKS
        tokens = u_all.shape[1]
        spot = lax.broadcasted_iota(jnp.int32, (slots, 1), 0).astype(F32)

        def fetch(g, slot):
            return pltpu.make_async_copy(u_all.at[pl.ds(g * BLOCKS, BLOCKS)], utile.at[slot], tin.at[slot])

        def put(g, slot):
            return pltpu.make_async_copy(otile.at[slot], fwd_ref.at[pl.ds(g * BLOCKS, BLOCKS)], tout.at[slot])

        fetch(0, 0).start()

        def step(g, carry):
            slot = g % 2
            fetch(g, slot).wait()

            @pl.when(g + 1 < steps)
            def _():
                fetch(g + 1, 1 - slot).start()
            for j in range(BLOCKS):
                p = g * BLOCKS + j
                lines = my_rows(meta[p // (side * CORES), (p // CORES) % side, p % CORES], experts, me, 0)
                pick = jnp.where(lines[0:1] == spot, 1.0, 0.0).astype(BF16)
                recv[pl.ds(j * slots, slots), :] = jnp.dot(pick, utile[slot, j], preferred_element_type=F32).astype(BF16)
            act = jnp.dot(recv[...], w13_ref[...], preferred_element_type=F32).astype(BF16).astype(F32)
            act_1, act_3 = act[:, :width], act[:, width:]
            hidden = (act_1 * jax.nn.sigmoid(act_1) * act_3).astype(BF16)

            @pl.when(g >= 2)
            def _():
                put(g - 2, slot).wait()
            otile[slot] = jnp.dot(hidden, w2_ref[...], preferred_element_type=F32).astype(BF16).reshape(BLOCKS, slots, 2 * half)
            put(g, slot).start()
            return carry

        lax.fori_loop(0, steps, step, 0)
        put(steps - 2, steps % 2).wait()
        put(steps - 1, 1 - steps % 2).wait()

    own_l.wait()
    own_r.wait()
    arrive(first)

    lane = lax.broadcasted_iota(jnp.int32, (1, slots), 1).astype(F32)
    row_ids = [y * peers + q for q in range(peers)]
    col_ids = [((q // CORES) * side + x) * CORES + q % CORES for q in range(peers)]

    def selector(ids):
        wide = meta.shape[-1]
        src = lax.broadcasted_iota(jnp.int32, (wide, wide), 0)
        dst = lax.broadcasted_iota(jnp.int32, (wide, wide), 1)
        hit = jnp.zeros((wide, wide), F32)
        for q, e in enumerate(ids):
            hit = jnp.where((src == offset + e) & (dst == q), 1.0, hit)
            hit = jnp.where((src == offset + experts + e) & (dst == peers + q), 1.0, hit)
        return hit.astype(BF16)

    sel_l, sel_r = selector(row_ids), selector(col_ids)

    def partial(block, sel, landed, sums, k):
        table = jnp.dot(block, sel, preferred_element_type=F32)
        weights = []
        for q in range(peers):
            scale = table[:, peers + q:peers + q + 1] if gated else 1.0
            weights.append(jnp.where(table[:, q:q + 1] == lane, scale, 0.0).astype(BF16))
        vals = landed[k].reshape(peers * slots, half)
        sums[k] = jnp.dot(jnp.concatenate(weights, axis=1), vals, preferred_element_type=F32)

    def sum_l(i):
        k = (y + i) % side
        partial(meta[k, x, core], sel_l, r1l, ps_l, k)

    def sum_r(i):
        k = (x + i) % side
        partial(meta[y, k, core], sel_r, r1r, ps_r, k)

    def send_l(i):
        yt = (y + i) % side
        return pltpu.make_async_remote_copy(src_ref=ps_l.at[yt], dst_ref=p2l.at[i], send_sem=s2.at[0, i], recv_sem=v2.at[0, i], device_id=dev(side, yt, x, core), device_id_type=MESH_ID)

    def send_r(i):
        xt = (x + i) % side
        return pltpu.make_async_remote_copy(src_ref=ps_r.at[xt], dst_ref=p2r.at[i], send_sem=s2.at[1, i], recv_sem=v2.at[1, i], device_id=dev(side, y, xt, core), device_id_type=MESH_ID)

    second = []
    for i in range(1, side):
        sum_l(i)
        if i > 1:
            second.append(send_r(i - 1))
            second[-1].start()
        sum_r(i)
        second.append(send_l(i))
        second[-1].start()
    sum_l(0)
    second.append(send_r(side - 1))
    second[-1].start()
    sum_r(0)
    sent(first)
    arrive(second)
    total_l = base_ref[:, :half].astype(F32) + ps_l[y]
    for i in range(1, side):
        total_l = total_l + p2l[i]
    out_ref[:, :half] = total_l.astype(BF16)
    total_r = base_ref[:, half:].astype(F32) + ps_r[x]
    for i in range(1, side):
        total_r = total_r + p2r[i]
    out_ref[:, half:] = total_r.astype(BF16)
    sent(second)


def run_combine(ident, out_slots, base, meta, offset, gated, extra=()):
    side = meta.shape[0]
    group, capacity, dim = out_slots.shape
    rows = base.shape[0]
    half = dim // 2
    peers = side * CORES
    cube = out_slots.reshape(side, side, CORES, capacity, dim)
    any_spec, vmem = pl.BlockSpec(memory_space=pl.ANY), pl.BlockSpec(memory_space=pltpu.VMEM)
    out_shape = [jax.ShapeDtypeStruct(base.shape, BF16)]
    in_specs = [any_spec, vmem, any_spec]
    out_specs = [vmem]
    scratch = [
        pltpu.VMEM(meta.shape, BF16),
        pltpu.VMEM((side, peers, capacity, half), BF16),
        pltpu.VMEM((side, peers, capacity, half), BF16),
        pltpu.VMEM((side, rows, half), F32),
        pltpu.VMEM((side, rows, half), F32),
        pltpu.VMEM((side, rows, half), F32),
        pltpu.VMEM((side, rows, half), F32),
        pltpu.SemaphoreType.DMA((3,)),
        pltpu.SemaphoreType.DMA((2, peers)),
        pltpu.SemaphoreType.DMA((2, peers)),
        pltpu.SemaphoreType.DMA((2, side)),
        pltpu.SemaphoreType.DMA((2, side)),
    ]
    if extra:
        in_specs += [any_spec, vmem, vmem]
        out_specs += [any_spec]
        out_shape += [jax.ShapeDtypeStruct(out_slots.shape, BF16)]
        scratch += [
            pltpu.VMEM((2, BLOCKS, rows, dim), BF16),
            pltpu.VMEM((BLOCKS * capacity, dim), BF16),
            pltpu.VMEM((2, BLOCKS, capacity, dim), BF16),
            pltpu.SemaphoreType.DMA((2,)),
            pltpu.SemaphoreType.DMA((2,)),
        ]
    return pl.pallas_call(
        functools.partial(combine_kernel, side, group, offset, gated, bool(extra)),
        out_shape=out_shape,
        in_specs=in_specs,
        out_specs=out_specs,
        scratch_shapes=scratch,
        compiler_params=pltpu.CompilerParams(collective_id=ident, has_side_effects=True, vmem_limit_bytes=64000000),
    )(cube, base, meta, *extra)


def solution(mesh):
    group = mesh.shape['expert']

    def local_step(x_a, x_b, dy_b, eid_a, slot_a, gate_a, eid_b, slot_b, gate_b, u_b, norm_1, norm_2, w_q, w_k, w_v, w_o, w_1, w_2, w_3):
        experts = w_1.shape[0] * group
        rows, model_dim = x_a.shape
        w1, w2, w3 = w_1[0], w_2[0], w_3[0]

        tables = slot_tables(eid_a, slot_a, gate_a, experts) + slot_tables(eid_b, slot_b, gate_b, experts)
        dy_ext = jnp.concatenate((dy_b,) + tables, axis=1)
        w13 = jnp.concatenate([w1, w3], axis=1)

        h_a = add_rows(x_a, attn_out(x_a, norm_1, w_q, w_k, w_v, w_o))
        u_a = rms_norm(h_a, norm_2)
        attn_val, attn_pull = jax.vjp(attn_out, x_b, norm_1, w_q, w_k, w_v, w_o)
        h_b = add_rows(x_b, attn_val)

        u_all, meta, grad_in, grad_w1, grad_w2, grad_w3 = run_backward(dy_ext, u_a, u_b[0], w13, w2, group)
        du, out_a = run_combine(1, grad_in, jnp.zeros_like(x_b), meta, 2 * experts, False, (u_all.reshape(group, rows, model_dim), w13, w2))
        y_a, = run_combine(2, out_a, h_a, meta, 0, True)

        _, norm_pull = jax.vjp(rms_norm, h_b, norm_2)
        dh_norm, g_n2 = norm_pull(du)
        dh = add_rows(dy_b, dh_norm)
        grad_x, g_n1, g_q, g_k, g_v, g_o = attn_pull(dh)
        dx_b = add_rows(dh, grad_x)
        grads = [g.astype(F32)[None] for g in (g_q, g_k, g_v, g_o, g_n1, g_n2)]
        return (y_a, dx_b, grad_w1[None], grad_w2[None], grad_w3[None], *grads)

    row_spec = P(('data', 'expert'), None)
    cube_spec = P(('data', 'expert'), None, None)
    quad_spec = P(('data', 'expert'), None, None, None)
    expert_spec = P('expert', None, None)
    in_specs = (row_spec, row_spec, row_spec, row_spec, row_spec, row_spec, row_spec, row_spec, row_spec, cube_spec, P(), P(), P(), P(), P(), P(), expert_spec, expert_spec, expert_spec)
    out_specs = (row_spec, row_spec, cube_spec, cube_spec, cube_spec, quad_spec, quad_spec, quad_spec, quad_spec, row_spec, row_spec)
    return jax.shard_map(local_step, mesh=mesh, in_specs=in_specs, out_specs=out_specs, check_vma=False)
```

time: 679 us -> 371 us (0.55)
  the two profiles are of different devices: /device:TPU:103 before, /device:TPU:97 now
where the time goes in v2:
time: 371 us; the launch traced here: 366 us
  Pallas kernels  303 us (82%)
  matrix products  30.6 us (8%)
  other arithmetic  19.1 us (5%)
  local copies, waits for them, and re-layouts  12 us (3%)
    pallas_call x2, Pallas kernels, run_combine(): pl.pallas_call(functools.partial(combine_kernel, side, group, offset, gat...  164 us
    pallas_call x1, Pallas kernels, run_backward(): pl.pallas_call(functools.partial(backward_kernel, side, group), out_shape...  139 us
    unnamed x9, matrix products  10.9 us
    unnamed x46, local copies, waits for them, and re-layouts  9.54 us

profile of v2, /device:TPU:97, one launch (start us, length us, event | category | flops | bytes accessed | tf_op | source)
XLA Modules:
  0.0 366.2 jit_solution(4138139543026572921)
XLA Ops:
  1.5 1.5 fusion.38
  3.0 2.7 bitcast_convert_fusion.4
  5.7 1.3 fusion.81
  7.1 4.7 %fusion.99 = (f32[8,2,256]{2,1,0:T(2,128)S(1)}, f32[8,2,256,256]{2,3,1,0:T(8,128)}) fusion(pred[256,256]{0,1:T(8,128)(4,1)S(1)} %iota_compare_fusion.1, bf16[256,8,2,64]{0,3,2,1:T(8,128)(2,1)} %bitcast.267, f32[256,8,64]{0,2,1:T(8,128)} %bitcast.268), kind=kOutput, calls=%fused_computation.150 | convolution fusion | flops 138543360 | bytes 5324800 | tf_op jit(solution)/shard_map/sub | solution.py:40
  11.7 1.8 fusion.83
  13.5 2.8 fusion.15
  18.1 1.0 fusion.35.u_ref
  19.8 1.2 concatenate.6.dy_ref
  21.0 3.1 pad_maximum_fusion.w13_ref.refs_4_
  24.1 139.3 %shard_map.266 = (bf16[4,4,2,256,1024]{4,3,2,1,0:T(8,128)(2,1)}, bf16[4,4,2,256,128]{4,3,2,1,0:T(8,128)(2,1)}, bf16[32,128,1024]{2,1,0:T(8,128)(2,1)}, f32[1024,...) custom-call(bf16[256,1152]{1,0:T(8,128)(2,1)} %concatenate.6.dy_ref, bf16[256,1024]{1,0:T(8,128)(2,1)} %fusion.35.u_ref, ...), custom_call_target="tpu_custom_call" | custom-call | tf_op jit(solution)/shard_map/pallas_call | solution.py:248
  164.3 81.5 %shard_map.267 = (bf16[256,1024]{1,0:T(8,128)(2,1)}, bf16[32,128,1024]{2,1,0:T(8,128)(2,1)}) custom-call(bf16[4,4,2,128,1024]{4,3,2,1,0:T(8,128)(2,1)} %bitcast.236, bf16[256,1024]{1,0:T(8,128)(2,1)} %broadcast_in_dim.142.refs_1_, bf16[4,4,2,256,128]{4,3,2,1,0:T(8,128)(2,1)} %get-tuple-element.20.refs_2_, bf16[32,256,1024]{2,1,0:T(8,128)(2,1)} %bitcast.231, ...), custom_call_target="tpu_custom_call" | custom-call | tf_op jit(solution)/shard_map/pallas_call | solution.py:455
  246.0 1.8 fusion.95
  254.8 2.7 bitcast_convert_fusion
  258.3 1.9 fusion.7
  260.3 1.7 fusion.5
  263.3 2.5 bitcast_convert_fusion.1
  267.1 1.5 bitcast_convert_fusion.2
  269.8 1.5 bitcast_convert_fusion.3
  273.4 1.2 add_convert_fusion
  275.7 82.4 %shard_map.268 = bf16[256,1024]{1,0:T(8,128)(2,1)} custom-call(bf16[4,4,2,128,1024]{4,3,2,1,0:T(8,128)(2,1)} %bitcast.233, bf16[256,1024]{1,0:T(8,128)(2,1)} %copy-done.4, bf16[4,4,2,256,128]{4,3,2,1,0:T(8,128)(2,1)} %get-tuple-element.20.refs_2_), custom_call_target="tpu_custom_call" | custom-call | tf_op jit(solution)/shard_map/pallas_call | solution.py:455
  358.1 2.0 copy.68
  360.1 3.2 copy.69
  363.4 1.3 copy.70
  364.7 1.3 copy.71
  (91 shorter events, 19.1 us)
Async XLA Ops:
  0.6 2.4 copy-start
  0.7 5.0 %copy-start.10 = (bf16[256,1024]{1,0:T(8,128)(2,1)S(1)}, bf16[256,1024]{1,0:T(8,128)(2,1)}, u32[]{:S(2)}) copy-start(bf16[256,1024]{1,0:T(8,128)(2,1)} %param.19) | copy-start | bytes 1572868
  0.7 5.0 %copy-start.19 = (bf16[1024,8,64]{0,2,1:T(8,128)(2,1)S(1)}, bf16[1024,8,64]{0,2,1:T(8,128)(2,1)}, u32[]{:S(2)}) copy-start(bf16[1024,8,64]{0,2,1:T(8,128)(2,1)} %param.32) | copy-start | bytes 3145732
  13.5 2.9 copy-start.2
  13.5 3.8 %copy-start.17 = (bf16[1024]{0:T(1024)(128)(2,1)S(1)}, bf16[1024]{0:T(1024)(128)(2,1)}, u32[]{:S(2)}) copy-start(bf16[1024]{0:T(1024)(128)(2,1)} %param.30) | copy-start | bytes 6148
  16.4 2.7 copy-start.13
  16.4 2.7 copy-start.11
  16.4 2.8 copy-start.14
  16.4 2.9 copy-start.12
  16.4 3.0 copy-start.15
  16.4 3.2 copy-start.16
  16.4 3.4 copy-start.5
  17.3 0.8 copy-start.4
  164.3 81.5 %copy-start.1 = (bf16[256,1024]{1,0:T(8,128)(2,1)S(1)}, bf16[256,1024]{1,0:T(8,128)(2,1)}, u32[]{:S(2)}) copy-start(bf16[256,1024]{1,0:T(8,128)(2,1)} %param.20) | copy-start | bytes 1572868
  250.3 1.2 copy-start.18
  251.5 1.6 copy-start.3
  251.5 2.4 copy-start.7
  252.1 2.4 copy-start.6
  271.3 1.2 copy-start.20
  358.1 5.3 %copy-start.9 = (f32[512,1024]{1,0:T(8,128)S(1)}, f32[512,1024]{1,0:T(8,128)}, u32[]{:S(2)}) copy-start(f32[512,1024]{1,0:T(8,128)} %get-tuple-element.25) | copy-start | bytes 6291460
  360.1 4.6 %copy-start.8 = (f32[1024,512]{1,0:T(8,128)S(1)}, f32[1024,512]{1,0:T(8,128)}, u32[]{:S(2)}) copy-start(f32[1024,512]{1,0:T(8,128)} %get-tuple-element.26) | copy-start | bytes 6291460

commit v3 on v2

--- a/solution.py
+++ b/solution.py
@@ -14,40 +14,18 @@
 MESH_ID = pl.DeviceIdType.MESH
 
 
-def rms_norm(values, gain):
-    wide = values.astype(jnp.float32)
-    scaled = wide * lax.rsqrt(jnp.mean(wide * wide, axis=-1, keepdims=True) + NORM_EPS)
-    return (scaled * gain.astype(jnp.float32)).astype(jnp.bfloat16)
-
-
-def add_rows(first, second):
-    return (first.astype(jnp.float32) + second.astype(jnp.float32)).astype(jnp.bfloat16)
-
-
-def attn_out(x_rows, norm_gain, w_q, w_k, w_v, w_o):
-    tokens = x_rows.shape[0]
-    heads = w_q.shape[1]
-    kv_heads = w_k.shape[1]
-    head_dim = w_q.shape[2]
-    normed = rms_norm(x_rows, norm_gain)
-    query = jnp.einsum('td,dhe->the', normed, w_q, preferred_element_type=jnp.float32).astype(jnp.bfloat16)
-    query = query.reshape(tokens, kv_heads, heads // kv_heads, head_dim)
-    key_proj = jnp.einsum('td,dge->tge', normed, w_k, preferred_element_type=jnp.float32).astype(jnp.bfloat16)
-    val_proj = jnp.einsum('td,dge->tge', normed, w_v, preferred_element_type=jnp.float32).astype(jnp.bfloat16)
-    scores = jnp.einsum('tgre,mge->grtm', query, key_proj, preferred_element_type=jnp.float32) * head_dim ** -0.5
-    causal = jnp.arange(tokens)[:, None] >= jnp.arange(tokens)[None, :]
-    scores = jnp.where(causal, scores, -1e30)
-    probs = jax.nn.softmax(scores, axis=-1).astype(jnp.bfloat16)
-    context = jnp.einsum('grtm,mge->tgre', probs, val_proj, preferred_element_type=jnp.float32).astype(jnp.bfloat16)
-    context = context.reshape(tokens, heads, head_dim)
-    return jnp.einsum('the,hed->td', context, w_o, preferred_element_type=jnp.float32).astype(jnp.bfloat16)
-
-
-def slot_tables(eid, slot, gate, experts):
-    hit = eid[:, :, None] == jnp.arange(experts)[None, None, :]
-    slots = jnp.sum(jnp.where(hit, slot[:, :, None] + 1, 0), axis=1) - 1
-    gates = jnp.sum(jnp.where(hit, gate[:, :, None].astype(F32), 0.0), axis=1)
-    return slots.astype(BF16), gates.astype(BF16)
+def slot_table(routes, experts):
+    choices, rows = routes[0].shape
+    columns = [part[...].astype(F32).T for part in routes]
+    lane = lax.broadcasted_iota(jnp.int32, (rows, 4 * experts), 1).astype(F32)
+    table = jnp.zeros(lane.shape, F32)
+    for i in range(2):
+        for j in range(choices):
+            eid, slot, gate = [columns[3 * i + k][:, j:j + 1] for k in range(3)]
+            spot = eid + 2.0 * i * experts
+            table = jnp.where(lane == spot, slot + 1.0, table)
+            table = jnp.where(lane == spot + experts, gate, table)
+    return table.astype(BF16)
 
 
 def place_of(side_x):
@@ -77,22 +55,59 @@
         y, x, c, side = self.y, self.x, self.core, self.side
         up, down, far = (y + 1) % side, (y + side - 1) % side, (y + 2) % side
         east, west, over = (x + 1) % side, (x + side - 1) % side, (x + 2) % side
-        pair = side // 2
-        lo, hi, every = pl.ds(0, pair), pl.ds(pair, pair), pl.ds(0, side)
+        every = pl.ds(0, side)
         twin = 1 - c
         L, R = self.left, self.right
-        self.own = []
-        for k in (1, side - 1, 2):
-            self.own.append(self.make((y, x, c, L), (y, (x + k) % side, c)))
-            self.own.append(self.make((y, x, c, R), ((y + k) % side, x, c)))
-        self.line = [self.make((y, every, c, L), (up, x, c)), self.make((every, x, c, R), (y, east, c)),
-                     self.make((y, every, c, L), (down, x, c)), self.make((every, x, c, R), (y, west, c))]
-        self.relay = [self.make((down, lo, c, L), (up, x, c)), self.make((lo, west, c, R), (y, east, c)),
-                      self.make((up, hi, c, L), (down, x, c)), self.make((hi, east, c, R), (y, west, c))]
+        self.own, self.line, self.relay = [], [], []
+        for k in range(1, side):
+            self.own.append([self.make((y, x, c, L), (y, (x + k) % side, c)), self.make((y, x, c, R), ((y + k) % side, x, c))])
+        for k in range(side):
+            xx, yy = (x + side - k) % side, (y + side - k) % side
+            self.line.append([self.make((y, xx, c, L), (up, x, c)), self.make((yy, x, c, R), (y, east, c)),
+                              self.make((y, xx, c, L), (down, x, c)), self.make((yy, x, c, R), (y, west, c))])
+        for k in range(side):
+            xx, yy = (x + side - k) % side, (y + side - k) % side
+            if k < 2:
+                self.relay.append([self.make((down, xx, c, L), (up, x, c)), self.make((yy, west, c, R), (y, east, c))])
+            else:
+                self.relay.append([self.make((up, xx, c, L), (down, x, c)), self.make((yy, east, c, R), (y, west, c))])
         self.twin_own = [self.make((y, every, c, L), (y, x, twin)), self.make((every, x, c, R), (y, x, twin))]
         self.twin_line = [self.make((up, every, c, L), (y, x, twin)), self.make((every, east, c, R), (y, x, twin)),
                           self.make((down, every, c, L), (y, x, twin)), self.make((every, west, c, R), (y, x, twin))]
         self.twin_far = [self.make((far, every, c, L), (y, x, twin)), self.make((every, over, c, R), (y, x, twin))]
+
+    def owns(self):
+        for k in (0, 2, 1):
+            start(self.own[k])
+
+    def lines(self):
+        for k in (1, 3, 2):
+            arrive(self.own[k - 1])
+            start(self.line[k])
+        start(self.twin_own)
+
+    def relays(self, order):
+        for k in order:
+            arrive(self.line[k][:2] if k < 2 else self.line[k][2:])
+            start(self.relay[k])
+
+    def rest_of_lines(self):
+        for k in (2, 3):
+            arrive(self.line[k][:2])
+        for k in (0, 1):
+            arrive(self.line[k][2:])
+        start(self.twin_line)
+
+    def fars(self):
+        for k in range(self.side):
+            arrive(self.relay[k])
+        start(self.twin_far)
+
+    def finish(self):
+        arrive(self.twin_own + self.twin_line + self.twin_far)
+
+    def drain(self):
+        sent(sum(self.own + self.line + self.relay, []) + self.twin_own + self.twin_line + self.twin_far)
 
     def make(self, spot, target):
         yy, xx, cc, cols = spot
@@ -102,7 +117,7 @@
         return pltpu.make_async_remote_copy(src_ref=part, dst_ref=part, send_sem=self.send.at[i], recv_sem=self.recv.at[i], device_id=dev(self.side, *target), device_id_type=MESH_ID)
 
 
-GATHER_COPIES = 22
+GATHER_COPIES = 38
 
 
 def start(copies):
@@ -127,70 +142,201 @@
     return lax.dot_general(jnp.where(pick, 1.0, 0.0).astype(BF16), table, (((1,), (1,)), ((), ())), preferred_element_type=F32)
 
 
+def scaled_rows(wide, gain):
+    scaled = wide * lax.rsqrt(jnp.mean(wide * wide, axis=-1, keepdims=True) + NORM_EPS)
+    return (scaled * gain).astype(BF16)
+
+
+def head_pair_probs(q_pair, k_head):
+    tokens, head_dim = k_head.shape
+    scores = lax.dot_general(q_pair, k_head, (((1,), (1,)), ((), ())), preferred_element_type=F32) * head_dim ** -0.5
+    row = lax.broadcasted_iota(jnp.int32, (tokens, tokens), 0)
+    col = lax.broadcasted_iota(jnp.int32, (tokens, tokens), 1)
+    causal = row >= col
+    scores = jnp.where(jnp.concatenate([causal, causal], axis=0), scores, -1e30)
+    weights = jnp.exp(scores - jnp.max(scores, axis=-1, keepdims=True))
+    return weights / jnp.sum(weights, axis=-1, keepdims=True)
+
+
+def attention_rows(x_ref, gain, wq, wk, wv, wo, head_dim, q_s, k_s, v_s, ctx_s, normed_s):
+    tokens = x_ref.shape[0]
+    normed_s[...] = scaled_rows(x_ref[...].astype(F32), gain)
+    q_s[...] = jnp.dot(normed_s[...], wq[...], preferred_element_type=F32).astype(BF16)
+    k_s[...] = jnp.dot(normed_s[...], wk[...], preferred_element_type=F32).astype(BF16)
+    v_s[...] = jnp.dot(normed_s[...], wv[...], preferred_element_type=F32).astype(BF16)
+    pack = 2 * head_dim
+
+    def pair(m, carry):
+        k_two = k_s[:, pl.ds(m * pack, pack)]
+        v_two = v_s[:, pl.ds(m * pack, pack)]
+        for j in range(2):
+            cols = pl.ds((2 * m + j) * pack, pack)
+            q_two = q_s[:, cols]
+            q_pair = jnp.concatenate([q_two[:, :head_dim], q_two[:, head_dim:]], axis=0)
+            k_head = k_two[:, j * head_dim:(j + 1) * head_dim]
+            v_head = v_two[:, j * head_dim:(j + 1) * head_dim]
+            probs = head_pair_probs(q_pair, k_head).astype(BF16)
+            ctx = jnp.dot(probs, v_head, preferred_element_type=F32).astype(BF16)
+            ctx_s[:, cols] = jnp.concatenate([ctx[:tokens], ctx[tokens:]], axis=1)
+        return carry
+
+    lax.fori_loop(0, k_s.shape[1] // pack, pair, 0)
+    return jnp.dot(ctx_s[...], wo[...], preferred_element_type=F32)
+
+
+NT = (((1,), (1,)), ((), ()))
+TN = (((0,), (0,)), ((), ()))
+
+
+def norm_pull(wide, gain, grad):
+    scale = lax.rsqrt(jnp.mean(wide * wide, axis=-1, keepdims=True) + NORM_EPS)
+    grad_gain = jnp.sum(grad * (wide * scale), axis=0, keepdims=True)
+    lifted = grad * gain
+    pull = lifted * scale - wide * (scale * scale * scale * jnp.mean(lifted * wide, axis=-1, keepdims=True))
+    return pull.astype(BF16), grad_gain.astype(BF16).astype(F32)
+
+
+def attention_backward(head_dim, x_ref, dy_ref, du_ref, gains_ref, wq, wk, wv, wo, dx_ref, gq, gk, gv, go, gn, q_s, k_s, v_s, ctx_s, normed_s, dctx_s, dq_s, dk_s, dv_s, dh_s):
+    tokens = x_ref.shape[0]
+    gain_1, gain_2 = gains_ref[0:1].astype(F32), gains_ref[1:2].astype(F32)
+    attn = attention_rows(x_ref, gain_1, wq, wk, wv, wo, head_dim, q_s, k_s, v_s, ctx_s, normed_s)
+    h = (x_ref[...].astype(F32) + attn.astype(BF16).astype(F32)).astype(BF16)
+    pulled, grad_gain = norm_pull(h.astype(F32), gain_2, du_ref[...].astype(F32))
+    gn[1:2, :] = grad_gain
+    dh_s[...] = (dy_ref[...].astype(F32) + pulled.astype(F32)).astype(BF16)
+    dctx_s[...] = lax.dot_general(dh_s[...], wo[...], NT, preferred_element_type=F32).astype(BF16)
+    go[...] = lax.dot_general(ctx_s[...], dh_s[...], TN, preferred_element_type=F32).astype(BF16)
+    pack = 2 * head_dim
+
+    def stack(two):
+        return jnp.concatenate([two[:, :head_dim], two[:, head_dim:]], axis=0)
+
+    def pair(m, carry):
+        tile = pl.ds(m * pack, pack)
+        k_two, v_two = k_s[:, tile], v_s[:, tile]
+        dk, dv = [], []
+        for j in range(2):
+            cols = pl.ds((2 * m + j) * pack, pack)
+            q_pair, dctx_pair = stack(q_s[:, cols]), stack(dctx_s[:, cols])
+            k_head = k_two[:, j * head_dim:(j + 1) * head_dim]
+            v_head = v_two[:, j * head_dim:(j + 1) * head_dim]
+            probs = head_pair_probs(q_pair, k_head)
+            dprobs = lax.dot_general(dctx_pair, v_head, NT, preferred_element_type=F32).astype(BF16).astype(F32)
+            dv.append(lax.dot_general(probs.astype(BF16), dctx_pair, TN, preferred_element_type=F32).astype(BF16))
+            dscores = probs * (dprobs - jnp.sum(dprobs * probs, axis=-1, keepdims=True))
+            dscores = (dscores * head_dim ** -0.5).astype(BF16)
+            dq = jnp.dot(dscores, k_head, preferred_element_type=F32).astype(BF16)
+            dq_s[:, cols] = jnp.concatenate([dq[:tokens], dq[tokens:]], axis=1)
+            dk.append(lax.dot_general(dscores, q_pair, TN, preferred_element_type=F32).astype(BF16))
+        dk_s[:, tile] = jnp.concatenate(dk, axis=1)
+        dv_s[:, tile] = jnp.concatenate(dv, axis=1)
+        return carry
+
+    lax.fori_loop(0, k_s.shape[1] // pack, pair, 0)
+    for grad, source in ((gq, dq_s), (gk, dk_s), (gv, dv_s)):
+        grad[...] = lax.dot_general(normed_s[...], source[...], TN, preferred_element_type=F32).astype(BF16)
+    dnormed = sum(lax.dot_general(source[...], weight[...], NT, preferred_element_type=F32) for source, weight in ((dq_s, wq), (dk_s, wk), (dv_s, wv)))
+    pulled, grad_gain = norm_pull(x_ref[...].astype(F32), gain_1, dnormed.astype(BF16).astype(F32))
+    gn[0:1, :] = grad_gain
+    dx_ref[...] = (dh_s[...].astype(F32) + pulled.astype(F32)).astype(BF16)
+
+
 BLOCKS = 4
 
 
-def backward_kernel(side, experts, dy_ref, u_ref, ub_ref, w13_ref, w2_ref, u_all, meta_all, du_ref, gw1, gw2, gw3, buf, w13t, w2t, tile, dout, acts, dtile, loc, tin, tout, sa, ra, sb, rb):
+def backward_kernel(side, experts, head_dim, dy_ref, x_ref, eid_a, slot_a, gate_a, eid_b, slot_b, gate_b, ub_ref, w1_ref, w2_ref, w3_ref, gains_ref, wq_ref, wk_ref, wv_ref, wo_ref, u_all, meta_all, du_ref, gw1, gw2, gw3, h_ref, buf, w13, w13t, w2t, tile, dout, acts, dtile, u_ref, loc, tin, tout, sa, ra, sb, rb):
     me, y, x, core = place_of(side)
     partners = [dev(side, y, (x + k) % side, core) for k in range(1, side)]
     partners += [dev(side, (y + k) % side, x, core) for k in range(1, side)]
     partners += [dev(side, y, x, 1 - core)]
+    dim = x_ref.shape[-1]
+    width = w2_ref.shape[0]
+    own_dy = pltpu.make_async_copy(dy_ref, buf.at[y, x, core, :, pl.ds(0, dim)], loc.at[0])
+    own_u = pltpu.make_async_copy(u_ref, u_all.at[y, x, core], loc.at[1])
     greet(partners)
-    dim = u_ref.shape[-1]
-    width = w2_ref.shape[0]
-    own_dy = pltpu.make_async_copy(dy_ref, buf.at[y, x, core], loc.at[0])
-    own_u = pltpu.make_async_copy(u_ref, u_all.at[y, x, core], loc.at[1])
     own_dy.start()
-    own_u.start()
+    buf[y, x, core, :, dim:] = slot_table((eid_a, slot_a, gate_a, eid_b, slot_b, gate_b), experts)
     first = Gather(side, buf, dim // 2, sa, ra)
     second = Gather(side, u_all, dim // 2 + dim // 8, sb, rb)
     own_dy.wait()
-    start(first.own)
-    w13t[...] = w13_ref[...].T
+    first.owns()
+    start(first.line[0])
+    tokens = x_ref.shape[0]
+    kv = wk_ref.shape[1]
+    attn = attention_rows(x_ref, gains_ref[0:1].astype(F32), wq_ref, wk_ref, wv_ref, wo_ref, head_dim, acts.at[pl.ds(0, tokens)], dout.at[pl.ds(0, tokens), pl.ds(0, kv)], dout.at[pl.ds(0, tokens), pl.ds(kv, kv)], acts.at[pl.ds(tokens, tokens)], dout.at[pl.ds(tokens, tokens)])
+    h_ref[...] = (x_ref[...].astype(F32) + attn.astype(BF16).astype(F32)).astype(BF16)
+    u_ref[...] = scaled_rows(h_ref[...].astype(F32), gains_ref[1:2].astype(F32))
+    own_u.start()
+    first.lines()
+    w13[:, :width] = w1_ref[...]
+    w13[:, width:] = w3_ref[...]
+    w13t[...] = w13[...].T
     w2t[...] = w2_ref[...].T
     gw1[...] = jnp.zeros_like(gw1)
     gw2[...] = jnp.zeros_like(gw2)
     gw3[...] = jnp.zeros_like(gw3)
     own_u.wait()
-    arrive(first.own)
-    start(first.line)
-    start(first.twin_own)
-    arrive(first.line)
-    start(first.relay)
-    start(first.twin_line)
-    start(second.own)
-    arrive(first.relay)
-    start(first.twin_far)
-    arrive(first.twin_own + first.twin_line + first.twin_far)
+    second.owns()
+    first.relays((0, 1, 3, 2))
+    start(second.line[0])
+    first.rest_of_lines()
+    arrive(first.twin_own + first.twin_line)
 
     slots = du_ref.shape[1]
     group = du_ref.shape[0]
     rows = BLOCKS * slots
     steps = group // BLOCKS
 
+    def turn(g):
+        far = jnp.where(g < 3, 0, jnp.where(g < 6, 1, g - 6))
+        near = jnp.where(g < 3, g, jnp.where(g < 6, g - 3, 3))
+        near = near + jnp.where(near == 2, 1, 0) - jnp.where(near == 3, 1, 0)
+        pair = x // 2
+        return ((y + near) % side) * (side // 2) + jnp.where(far == 1, 1 - pair, pair)
+
     def fetch(g, slot):
-        return pltpu.make_async_copy(ub_ref.at[pl.ds(g * rows, rows)], tile.at[slot], tin.at[slot])
+        return pltpu.make_async_copy(ub_ref.at[pl.ds(turn(g) * rows, rows)], tile.at[slot], tin.at[slot])
 
     def put(g, slot):
-        return pltpu.make_async_copy(dtile.at[slot], du_ref.at[pl.ds(g * BLOCKS, BLOCKS)], tout.at[slot])
+        return pltpu.make_async_copy(dtile.at[slot], du_ref.at[pl.ds(turn(g) * BLOCKS, BLOCKS)], tout.at[slot])
 
     fetch(0, 0).start()
-    spot = lax.broadcasted_iota(jnp.int32, (slots, 1), 0).astype(F32)
+    spot = lax.broadcasted_iota(jnp.int32, (slots, 1), 0).astype(F32) + 1.0
 
     def step(g, carry):
         slot = g % 2
+
+        @pl.when(g == 1)
+        def _():
+            second.lines()
+
+        @pl.when(g == 2)
+        def _():
+            first.fars()
+
+        @pl.when(g == 3)
+        def _():
+            arrive(first.twin_far)
+
+        @pl.when(g == 6)
+        def _():
+            second.relays((0, 1))
+
+        @pl.when(g == 7)
+        def _():
+            second.relays((3,))
         fetch(g, slot).wait()
 
         @pl.when(g + 1 < steps)
         def _():
             fetch(g + 1, 1 - slot).start()
         for j in range(BLOCKS):
-            p = g * BLOCKS + j
+            p = turn(g) * BLOCKS + j
             block = buf.at[p // (side * CORES), (p // CORES) % side, p % CORES]
             lines = my_rows(block[:, dim:], experts, me, 2 * experts)
             pick = jnp.where(lines[0:1] == spot, lines[1:2], 0.0).astype(BF16)
             dout[pl.ds(j * slots, slots), :] = jnp.dot(pick, block[:, :dim], preferred_element_type=F32).astype(BF16)
-        pre = jnp.dot(tile[slot], w13_ref[...], preferred_element_type=F32).astype(BF16).astype(F32)
+        pre = jnp.dot(tile[slot], w13[...], preferred_element_type=F32).astype(BF16).astype(F32)
         pre_1, pre_3 = pre[:, :width], pre[:, width:]
         sigma = jax.nn.sigmoid(pre_1)
         silu_1 = pre_1 * sigma
@@ -210,43 +356,32 @@
         both = lax.dot_general(tile[slot], acts[...], over, preferred_element_type=F32)
         gw1[...] += both[:, :width]
         gw3[...] += both[:, width:]
-
-        @pl.when(g == 1)
-        def _():
-            arrive(second.own)
-            start(second.line)
-            start(second.twin_own)
-
-        @pl.when(g == 6)
-        def _():
-            arrive(second.line)
-            start(second.relay)
-            start(second.twin_line)
         return carry
 
     lax.fori_loop(0, steps, step, 0)
+    second.relays((2,))
+    second.rest_of_lines()
+    second.fars()
     meta_out = pltpu.make_async_copy(buf.at[:, :, :, :, pl.ds(dim, buf.shape[-1] - dim)], meta_all, loc.at[0])
     meta_out.start()
     put(steps - 2, steps % 2).wait()
     put(steps - 1, 1 - steps % 2).wait()
-    arrive(second.relay)
-    start(second.twin_far)
-    arrive(second.twin_own + second.twin_line + second.twin_far)
-    for gather in (first, second):
-        sent(gather.own + gather.line + gather.relay + gather.twin_own + gather.twin_line + gather.twin_far)
+    second.finish()
+    first.drain()
+    second.drain()
     meta_out.wait()
 
 
-def run_backward(dy_ext, u_a, saved, w13, w2, group):
+def run_backward(dy, x_a, routes, saved, weights, head_dim, group):
     side = int(round((group // CORES) ** 0.5))
-    rows, dim = u_a.shape
-    wide = dy_ext.shape[1]
+    rows, dim = x_a.shape
+    wide = dim + 4 * group
     slots = saved.shape[0] // group
-    width = w2.shape[0]
+    width = weights[1].shape[0]
     tall = BLOCKS * slots
     any_spec, vmem = pl.BlockSpec(memory_space=pl.ANY), pl.BlockSpec(memory_space=pltpu.VMEM)
     return pl.pallas_call(
-        functools.partial(backward_kernel, side, group),
+        functools.partial(backward_kernel, side, group, head_dim),
         out_shape=[
             jax.ShapeDtypeStruct((side, side, CORES, rows, dim), BF16),
             jax.ShapeDtypeStruct((side, side, CORES, rows, wide - dim), BF16),
@@ -254,30 +389,37 @@
             jax.ShapeDtypeStruct((dim, width), F32),
             jax.ShapeDtypeStruct((width, dim), F32),
             jax.ShapeDtypeStruct((dim, width), F32),
+            jax.ShapeDtypeStruct((rows, dim), BF16),
         ],
-        in_specs=[any_spec, vmem, any_spec, vmem, vmem],
-        out_specs=[any_spec, any_spec, any_spec, vmem, vmem, vmem],
+        in_specs=[any_spec, vmem] + [vmem] * len(routes) + [any_spec] + [vmem] * len(weights),
+        out_specs=[any_spec, any_spec, any_spec, vmem, vmem, vmem, vmem],
         scratch_shapes=[
             pltpu.VMEM((side, side, CORES, rows, wide), BF16),
+            pltpu.VMEM((dim, 2 * width), BF16),
             pltpu.VMEM((2 * width, dim), BF16),
             pltpu.VMEM((dim, width), BF16),
             pltpu.VMEM((2, tall, dim), BF16),
             pltpu.VMEM((tall, dim), BF16),
             pltpu.VMEM((tall, 2 * width), BF16),
             pltpu.VMEM((2, BLOCKS, slots, dim), BF16),
+            pltpu.VMEM((rows, dim), BF16),
             pltpu.SemaphoreType.DMA((2,)),
             pltpu.SemaphoreType.DMA((2,)),
             pltpu.SemaphoreType.DMA((2,)),
         ] + [pltpu.SemaphoreType.DMA((GATHER_COPIES,))] * 4,
         compiler_params=pltpu.CompilerParams(collective_id=0, has_side_effects=True, vmem_limit_bytes=64000000),
-    )(dy_ext, u_a, saved, w13, w2)
-
-
-def combine_kernel(side, experts, offset, gated, forward, *refs):
+    )(dy, x_a, *routes, saved, *weights)
+
+
+def combine_kernel(side, experts, offset, gated, forward, head_dim, *refs):
     if forward:
-        o_ref, base_ref, meta_ref, u_all, w13_ref, w2_ref, out_ref, fwd_ref, meta, r1l, r1r, ps_l, ps_r, p2l, p2r, loc_sem, s1, v1, s2, v2, utile, recv, otile, tin, tout = refs
+        o_ref, base_ref, meta_ref, u_all, w1_ref, w2_ref, w3_ref, out_ref, fwd_ref, meta, r1l, r1r, ps_l, ps_r, p2l, p2r, loc_sem, s1, v1, s2, v2, utile, recv, otile, w13, tin, tout = refs
     else:
-        o_ref, base_ref, meta_ref, out_ref, meta, r1l, r1r, ps_l, ps_r, p2l, p2r, loc_sem, s1, v1, s2, v2 = refs
+        o_ref, base_ref, meta_ref = refs[:3]
+        attention_refs = refs[3:11] + refs[12:18]
+        attention_scratch = refs[-10:]
+        out_ref = refs[11]
+        meta, r1l, r1r, ps_l, ps_r, p2l, p2r, loc_sem, s1, v1, s2, v2 = refs[18:-10]
     me, y, x, core = place_of(side)
     peers = side * CORES
     q_row = x * CORES + core
@@ -308,7 +450,7 @@
         group = fwd_ref.shape[0]
         steps = group // BLOCKS
         tokens = u_all.shape[1]
-        spot = lax.broadcasted_iota(jnp.int32, (slots, 1), 0).astype(F32)
+        spot = lax.broadcasted_iota(jnp.int32, (slots, 1), 0).astype(F32) + 1.0
 
         def fetch(g, slot):
             return pltpu.make_async_copy(u_all.at[pl.ds(g * BLOCKS, BLOCKS)], utile.at[slot], tin.at[slot])
@@ -317,6 +459,8 @@
             return pltpu.make_async_copy(otile.at[slot], fwd_ref.at[pl.ds(g * BLOCKS, BLOCKS)], tout.at[slot])
 
         fetch(0, 0).start()
+        w13[:, :width] = w1_ref[...]
+        w13[:, width:] = w3_ref[...]
 
         def step(g, carry):
             slot = g % 2
@@ -330,7 +474,7 @@
                 lines = my_rows(meta[p // (side * CORES), (p // CORES) % side, p % CORES], experts, me, 0)
                 pick = jnp.where(lines[0:1] == spot, 1.0, 0.0).astype(BF16)
                 recv[pl.ds(j * slots, slots), :] = jnp.dot(pick, utile[slot, j], preferred_element_type=F32).astype(BF16)
-            act = jnp.dot(recv[...], w13_ref[...], preferred_element_type=F32).astype(BF16).astype(F32)
+            act = jnp.dot(recv[...], w13[...], preferred_element_type=F32).astype(BF16).astype(F32)
             act_1, act_3 = act[:, :width], act[:, width:]
             hidden = (act_1 * jax.nn.sigmoid(act_1) * act_3).astype(BF16)
 
@@ -344,12 +488,14 @@
         lax.fori_loop(0, steps, step, 0)
         put(steps - 2, steps % 2).wait()
         put(steps - 1, 1 - steps % 2).wait()
+    else:
+        attention_backward(head_dim, *attention_refs, *attention_scratch)
 
     own_l.wait()
     own_r.wait()
     arrive(first)
 
-    lane = lax.broadcasted_iota(jnp.int32, (1, slots), 1).astype(F32)
+    lane = lax.broadcasted_iota(jnp.int32, (1, slots), 1).astype(F32) + 1.0
     row_ids = [y * peers + q for q in range(peers)]
     col_ids = [((q // CORES) * side + x) * CORES + q % CORES for q in range(peers)]
 
@@ -416,7 +562,7 @@
     sent(second)
 
 
-def run_combine(ident, out_slots, base, meta, offset, gated, extra=()):
+def run_combine(ident, out_slots, base, meta, offset, gated, forward, head_dim, extra):
     side = meta.shape[0]
     group, capacity, dim = out_slots.shape
     rows = base.shape[0]
@@ -441,19 +587,26 @@
         pltpu.SemaphoreType.DMA((2, side)),
         pltpu.SemaphoreType.DMA((2, side)),
     ]
-    if extra:
-        in_specs += [any_spec, vmem, vmem]
+    if forward:
+        in_specs += [any_spec, vmem, vmem, vmem]
         out_specs += [any_spec]
         out_shape += [jax.ShapeDtypeStruct(out_slots.shape, BF16)]
         scratch += [
             pltpu.VMEM((2, BLOCKS, rows, dim), BF16),
             pltpu.VMEM((BLOCKS * capacity, dim), BF16),
             pltpu.VMEM((2, BLOCKS, capacity, dim), BF16),
+            pltpu.VMEM((dim, 2 * extra[2].shape[0]), BF16),
             pltpu.SemaphoreType.DMA((2,)),
             pltpu.SemaphoreType.DMA((2,)),
         ]
+    else:
+        in_specs += [vmem] * len(extra)
+        out_specs += [vmem] * 6
+        full, kv = extra[4].shape[1], extra[5].shape[1]
+        out_shape += [jax.ShapeDtypeStruct(base.shape, BF16)] + [jax.ShapeDtypeStruct(part.shape, BF16) for part in extra[4:]] + [jax.ShapeDtypeStruct((2, dim), F32)]
+        scratch += [pltpu.VMEM((rows, cols), BF16) for cols in (full, kv, kv, full, dim, full, full, kv, kv, dim)]
     return pl.pallas_call(
-        functools.partial(combine_kernel, side, group, offset, gated, bool(extra)),
+        functools.partial(combine_kernel, side, group, offset, gated, forward, head_dim),
         out_shape=out_shape,
         in_specs=in_specs,
         out_specs=out_specs,
@@ -470,25 +623,15 @@
         rows, model_dim = x_a.shape
         w1, w2, w3 = w_1[0], w_2[0], w_3[0]
 
-        tables = slot_tables(eid_a, slot_a, gate_a, experts) + slot_tables(eid_b, slot_b, gate_b, experts)
-        dy_ext = jnp.concatenate((dy_b,) + tables, axis=1)
-        w13 = jnp.concatenate([w1, w3], axis=1)
-
-        h_a = add_rows(x_a, attn_out(x_a, norm_1, w_q, w_k, w_v, w_o))
-        u_a = rms_norm(h_a, norm_2)
-        attn_val, attn_pull = jax.vjp(attn_out, x_b, norm_1, w_q, w_k, w_v, w_o)
-        h_b = add_rows(x_b, attn_val)
-
-        u_all, meta, grad_in, grad_w1, grad_w2, grad_w3 = run_backward(dy_ext, u_a, u_b[0], w13, w2, group)
-        du, out_a = run_combine(1, grad_in, jnp.zeros_like(x_b), meta, 2 * experts, False, (u_all.reshape(group, rows, model_dim), w13, w2))
-        y_a, = run_combine(2, out_a, h_a, meta, 0, True)
-
-        _, norm_pull = jax.vjp(rms_norm, h_b, norm_2)
-        dh_norm, g_n2 = norm_pull(du)
-        dh = add_rows(dy_b, dh_norm)
-        grad_x, g_n1, g_q, g_k, g_v, g_o = attn_pull(dh)
-        dx_b = add_rows(dh, grad_x)
-        grads = [g.astype(F32)[None] for g in (g_q, g_k, g_v, g_o, g_n1, g_n2)]
+        head_dim = w_q.shape[2]
+        gains = jnp.stack([norm_1, norm_2])
+        routes = tuple(part.T for part in (eid_a, slot_a, gate_a, eid_b, slot_b, gate_b))
+        flat = (w_q.reshape(model_dim, -1), w_k.reshape(model_dim, -1), w_v.reshape(model_dim, -1), w_o.reshape(-1, model_dim))
+
+        u_all, meta, grad_in, grad_w1, grad_w2, grad_w3, h_a = run_backward(dy_b, x_a, routes, u_b[0], (w1, w2, w3, gains) + flat, head_dim, group)
+        du, out_a = run_combine(1, grad_in, jnp.zeros_like(x_b), meta, 2 * experts, False, True, head_dim, (u_all.reshape(group, rows, model_dim), w1, w2, w3))
+        y_a, dx_b, g_q, g_k, g_v, g_o, g_n = run_combine(2, out_a, h_a, meta, 0, True, False, head_dim, (x_b, dy_b, du, gains) + flat)
+        grads = tuple(g.reshape(w.shape).astype(F32)[None] for g, w in ((g_q, w_q), (g_k, w_k), (g_v, w_v), (g_o, w_o))) + (g_n[0:1], g_n[1:2])
         return (y_a, dx_b, grad_w1[None], grad_w2[None], grad_w3[None], *grads)
 
     row_spec = P(('data', 'expert'), None)

time: 371 us -> 340 us (0.916)
  matrix products: 30.6 us -> 0 us
  other arithmetic: 19.1 us -> 3.09 us
  local copies, waits for them, and re-layouts: 12 us -> 26 us
    dot_general x14 -> x0, matrix products: 15.1 us -> none  [the longest x4 5.92 us: attn_out(): jnp.einsum('grtm,mge->tgre', probs, val_proj, preferred_element_type=jnp....]
    unnamed x9 -> x0, matrix products: 10.9 us -> none
    convert_element_type x2 -> x3, local copies, waits for them, and re-layouts: 0.24 us -> 8.43 us  [local_step(): g.reshape(w.shape).astype(F32)[None]]
    reshape x0 -> x3, local copies, waits for them, and re-layouts: none -> 6.28 us  [the longest x1 2.54 us: local_step(): w_q.reshape(model_dim, -1)]
    broadcast_in_dim x3 -> x0, other arithmetic: 5.45 us -> none  [local_step(): grads = [g.astype(F32)[None] for g in (g_q, g_k, g_v, g_o, g_n1, g_n2)]]
    sub x1 -> x0, matrix products: 4.66 us -> none  [attn_out(): probs = jax.nn.softmax(scores, axis=-1).astype(jnp.bfloat16)]
    unnamed x46 -> x23, local copies, waits for them, and re-layouts: 9.54 us -> 7.63 us
where the time goes in v3:
time: 340 us; the launch traced here: 334 us
  Pallas kernels  303 us (89%)
  local copies, waits for them, and re-layouts  26 us (8%)
    pallas_call x2, Pallas kernels, run_combine(): pl.pallas_call(functools.partial(combine_kernel, side, group, offset, gat...  167 us
    pallas_call x1, Pallas kernels, run_backward(): pl.pallas_call(functools.partial(backward_kernel, side, group, head_dim),...  136 us
    convert_element_type x3, local copies, waits for them, and re-layouts, local_step(): g.reshape(w.shape).astype(F32)[None]  8.43 us
    unnamed x23, local copies, waits for them, and re-layouts  7.63 us

profile of v3, /device:TPU:97, one launch (start us, length us, event | category | flops | bytes accessed | tf_op | source)
XLA Modules:
  0.0 333.7 jit_solution(8652190542576425430)
XLA Ops:
  0.6 0.0 copy-start.6
  0.7 0.8 stack.9
  1.4 0.7 stack.10
  2.1 0.6 pad_maximum_fusion.gains_ref.refs_6_
  2.7 2.4 copy.37.wk_ref.refs_8_
  5.1 0.0 copy-done.6
  5.1 1.3 copy.38.wv_ref.refs_9_
  6.5 2.5 copy.36.wq_ref.refs_7_
  9.0 136.1 %shard_map.266 = (bf16[4,4,2,256,1024]{4,3,2,1,0:T(8,128)(2,1)}, bf16[4,4,2,256,128]{4,3,2,1,0:T(8,128)(2,1)}, bf16[32,128,1024]{2,1,0:T(8,128)(2,1)}, f32[1024,...) custom-call(bf16[256,1024]{1,0:T(8,128)(2,1)} %refs_4_.1, ...), custom_call_target="tpu_custom_call" | custom-call | tf_op jit(solution)/shard_map/pallas_call | solution.py:383
  145.1 0.9 broadcast_in_dim.16.refs_1_
  146.0 81.0 %shard_map.267 = (bf16[256,1024]{1,0:T(8,128)(2,1)}, bf16[32,128,1024]{2,1,0:T(8,128)(2,1)}) custom-call(bf16[4,4,2,128,1024]{4,3,2,1,0:T(8,128)(2,1)} %bitcast.30, bf16[256,1024]{1,0:T(8,128)(2,1)} %broadcast_in_dim.16.refs_1_, bf16[4,4,2,256,128]{4,3,2,1,0:T(8,128)(2,1)} %get-tuple-element.28.refs_2_, bf16[32,256,1024]{2,1,0:T(8,128)(2,1)} %bitcast.25, ...), custom_call_target="tpu_custom_call" | custom-call | tf_op jit(solution)/shard_map/pallas_call | solution.py:608
  227.0 86.3 %shard_map.268 = (bf16[256,1024]{1,0:T(8,128)(2,1)}, bf16[256,1024]{1,0:T(8,128)(2,1)}, bf16[1024,1024]{1,0:T(8,128)(2,1)}, bf16[1024,512]{1,0:T(8,128)(2,1)}, b...) custom-call(bf16[4,4,2,128,1024]{4,3,2,1,0:T(8,128)(2,1)} %bitcast.29, ...), custom_call_target="tpu_custom_call" | custom-call | tf_op jit(solution)/shard_map/pallas_call | solution.py:608
  313.3 1.4 fusion
  314.7 2.6 copy.43
  317.3 1.6 copy.44
  318.9 4.3 %copy.42 = f32[1024,1024]{0,1:T(8,128)} copy(bf16[1024,1024]{1,0:T(8,128)(2,1)} %get-tuple-element.38) | data formatting | bytes 6291456 | tf_op jit(solution)/shard_map/convert_element_type | solution.py:634
  323.1 2.5 convert.4
  325.6 0.8 copy.50
  326.4 0.8 copy.51
  327.2 1.3 copy.52
  328.5 1.0 copy-done.3
  329.6 1.3 copy.53
  330.9 1.0 copy-done.2
  331.9 1.3 copy.54
  (14 shorter events, 0.0 us)
Async XLA Ops:
  0.6 4.5 %copy-start.6 = (bf16[1024,8,64]{0,2,1:T(8,128)(2,1)S(1)}, bf16[1024,8,64]{0,2,1:T(8,128)(2,1)}, u32[]{:S(2)}) copy-start(bf16[1024,8,64]{0,2,1:T(8,128)(2,1)} %param.33) | copy-start | bytes 3145732
  2.7 3.7 %copy-start.1 = (bf16[1024,16,64]{0,2,1:T(8,128)(2,1)S(1)}, bf16[1024,16,64]{0,2,1:T(8,128)(2,1)}, u32[]{:S(2)}) copy-start(bf16[1024,16,64]{0,2,1:T(8,128)(2,1)} %param.31) | copy-start | bytes 6291460
  313.3 4.0 %copy-start.5 = (bf16[1024,512]{1,0:T(8,128)(2,1)S(1)}, bf16[1024,512]{1,0:T(8,128)(2,1)}, u32[]{:S(2)}) copy-start(bf16[1024,512]{1,0:T(8,128)(2,1)} %get-tuple-element.40) | copy-start | bytes 3145732
  318.9 4.3 %copy-start = (bf16[1024,1024]{1,0:T(8,128)(2,1)S(1)}, bf16[1024,1024]{1,0:T(8,128)(2,1)}, u32[]{:S(2)}) copy-start(bf16[1024,1024]{1,0:T(8,128)(2,1)} %get-tuple-element.41) | copy-start | bytes 6291460
  323.1 2.5 copy-start.8
  323.1 3.3 copy-start.7
  323.1 4.1 %copy-start.4 = (f32[1024,512]{1,0:T(8,128)S(1)}, f32[1024,512]{1,0:T(8,128)}, u32[]{:S(2)}) copy-start(f32[1024,512]{1,0:T(8,128)} %get-tuple-element.35) | copy-start | bytes 6291460
  327.2 2.3 copy-start.3
  329.6 2.3 copy-start.2

commit v4 on v3

--- a/solution.py
+++ b/solution.py
@@ -196,12 +196,10 @@
     return pull.astype(BF16), grad_gain.astype(BF16).astype(F32)
 
 
-def attention_backward(head_dim, x_ref, dy_ref, du_ref, gains_ref, wq, wk, wv, wo, dx_ref, gq, gk, gv, go, gn, q_s, k_s, v_s, ctx_s, normed_s, dctx_s, dq_s, dk_s, dv_s, dh_s):
+def attention_backward(head_dim, x_ref, dy_ref, du_ref, gains_ref, wq, wk, wv, wo, dx_ref, gq, gk, gv, go, gn, q_s, k_s, v_s, ctx_s, normed_s, dctx_s, dq_s, dk_s, dv_s, dh_s, h_s):
     tokens = x_ref.shape[0]
     gain_1, gain_2 = gains_ref[0:1].astype(F32), gains_ref[1:2].astype(F32)
-    attn = attention_rows(x_ref, gain_1, wq, wk, wv, wo, head_dim, q_s, k_s, v_s, ctx_s, normed_s)
-    h = (x_ref[...].astype(F32) + attn.astype(BF16).astype(F32)).astype(BF16)
-    pulled, grad_gain = norm_pull(h.astype(F32), gain_2, du_ref[...].astype(F32))
+    pulled, grad_gain = norm_pull(h_s[...].astype(F32), gain_2, du_ref[...].astype(F32))
     gn[1:2, :] = grad_gain
     dh_s[...] = (dy_ref[...].astype(F32) + pulled.astype(F32)).astype(BF16)
     dctx_s[...] = lax.dot_general(dh_s[...], wo[...], NT, preferred_element_type=F32).astype(BF16)
@@ -411,215 +409,192 @@
     )(dy, x_a, *routes, saved, *weights)
 
 
-def combine_kernel(side, experts, offset, gated, forward, head_dim, *refs):
-    if forward:
-        o_ref, base_ref, meta_ref, u_all, w1_ref, w2_ref, w3_ref, out_ref, fwd_ref, meta, r1l, r1r, ps_l, ps_r, p2l, p2r, loc_sem, s1, v1, s2, v2, utile, recv, otile, w13, tin, tout = refs
-    else:
-        o_ref, base_ref, meta_ref = refs[:3]
-        attention_refs = refs[3:11] + refs[12:18]
-        attention_scratch = refs[-10:]
-        out_ref = refs[11]
-        meta, r1l, r1r, ps_l, ps_r, p2l, p2r, loc_sem, s1, v1, s2, v2 = refs[18:-10]
-    me, y, x, core = place_of(side)
-    peers = side * CORES
-    q_row = x * CORES + core
-    q_col = y * CORES + core
-    half = o_ref.shape[-1] // 2
-    slots = o_ref.shape[-2]
-    moves = [(k, dc) for k in range(1, side) for dc in range(CORES)] + [(0, 1)]
-    partners = [(y, (x + k) % side, (core + dc) % CORES) for k, dc in moves]
-    partners += [((y + k) % side, x, (core + dc) % CORES) for k, dc in moves if k]
-    greet([dev(side, *spot) for spot in partners])
-
-    first = []
-    for i, (k, dc) in enumerate(moves):
-        xt, yt, ct = (x + k) % side, (y + k) % side, (core + dc) % CORES
-        first.append(pltpu.make_async_remote_copy(src_ref=o_ref.at[:, xt, ct, :, pl.ds(0, half)], dst_ref=r1l.at[:, q_row], send_sem=s1.at[0, i], recv_sem=v1.at[0, i], device_id=dev(side, y, xt, ct), device_id_type=MESH_ID))
-        first.append(pltpu.make_async_remote_copy(src_ref=o_ref.at[yt, :, ct, :, pl.ds(half, half)], dst_ref=r1r.at[:, q_col], send_sem=s1.at[1, i], recv_sem=v1.at[1, i], device_id=dev(side, yt, x, ct), device_id_type=MESH_ID))
-    start(first)
-    own_l = pltpu.make_async_copy(o_ref.at[:, x, core, :, pl.ds(0, half)], r1l.at[:, q_row], loc_sem.at[0])
-    own_r = pltpu.make_async_copy(o_ref.at[y, :, core, :, pl.ds(half, half)], r1r.at[:, q_col], loc_sem.at[1])
-    meta_in = pltpu.make_async_copy(meta_ref, meta, loc_sem.at[2])
-    own_l.start()
-    own_r.start()
-    meta_in.start()
-    meta_in.wait()
-
-    if forward:
-        width = w2_ref.shape[0]
-        group = fwd_ref.shape[0]
-        steps = group // BLOCKS
-        tokens = u_all.shape[1]
-        spot = lax.broadcasted_iota(jnp.int32, (slots, 1), 0).astype(F32) + 1.0
-
-        def fetch(g, slot):
-            return pltpu.make_async_copy(u_all.at[pl.ds(g * BLOCKS, BLOCKS)], utile.at[slot], tin.at[slot])
-
-        def put(g, slot):
-            return pltpu.make_async_copy(otile.at[slot], fwd_ref.at[pl.ds(g * BLOCKS, BLOCKS)], tout.at[slot])
-
-        fetch(0, 0).start()
-        w13[:, :width] = w1_ref[...]
-        w13[:, width:] = w3_ref[...]
-
-        def step(g, carry):
-            slot = g % 2
-            fetch(g, slot).wait()
-
-            @pl.when(g + 1 < steps)
-            def _():
-                fetch(g + 1, 1 - slot).start()
-            for j in range(BLOCKS):
-                p = g * BLOCKS + j
-                lines = my_rows(meta[p // (side * CORES), (p // CORES) % side, p % CORES], experts, me, 0)
-                pick = jnp.where(lines[0:1] == spot, 1.0, 0.0).astype(BF16)
-                recv[pl.ds(j * slots, slots), :] = jnp.dot(pick, utile[slot, j], preferred_element_type=F32).astype(BF16)
-            act = jnp.dot(recv[...], w13[...], preferred_element_type=F32).astype(BF16).astype(F32)
-            act_1, act_3 = act[:, :width], act[:, width:]
-            hidden = (act_1 * jax.nn.sigmoid(act_1) * act_3).astype(BF16)
-
-            @pl.when(g >= 2)
-            def _():
-                put(g - 2, slot).wait()
-            otile[slot] = jnp.dot(hidden, w2_ref[...], preferred_element_type=F32).astype(BF16).reshape(BLOCKS, slots, 2 * half)
-            put(g, slot).start()
-            return carry
-
-        lax.fori_loop(0, steps, step, 0)
-        put(steps - 2, steps % 2).wait()
-        put(steps - 1, 1 - steps % 2).wait()
-    else:
-        attention_backward(head_dim, *attention_refs, *attention_scratch)
-
-    own_l.wait()
-    own_r.wait()
-    arrive(first)
-
-    lane = lax.broadcasted_iota(jnp.int32, (1, slots), 1).astype(F32) + 1.0
-    row_ids = [y * peers + q for q in range(peers)]
-    col_ids = [((q // CORES) * side + x) * CORES + q % CORES for q in range(peers)]
-
-    def selector(ids):
-        wide = meta.shape[-1]
+class Return:
+    def __init__(self, side, experts, offset, gated, slots_ref, meta, bufs, sems):
+        self.side, self.experts, self.offset, self.gated, self.src, self.meta = side, experts, offset, gated, slots_ref, meta
+        self.r1l, self.r1r, self.ps_l, self.ps_r, self.p2l, self.p2r = bufs
+        self.loc, self.s1, self.v1, self.s2, self.v2 = sems
+        _, y, x, core = self.spot = place_of(side)
+        self.peers = side * CORES
+        self.slots, self.half = slots_ref.shape[-2], slots_ref.shape[-1] // 2
+        half = self.half
+        self.first, self.second_l, self.second_r = [], [], []
+        q_row, q_col = x * CORES + core, y * CORES + core
+        for i, (k, dc) in enumerate(return_moves(side)):
+            xt, yt, ct = (x + k) % side, (y + k) % side, (core + dc) % CORES
+            self.first.append(pltpu.make_async_remote_copy(src_ref=slots_ref.at[:, xt, ct, :, pl.ds(0, half)], dst_ref=self.r1l.at[:, q_row], send_sem=self.s1.at[0, i], recv_sem=self.v1.at[0, i], device_id=dev(side, y, xt, ct), device_id_type=MESH_ID))
+            self.first.append(pltpu.make_async_remote_copy(src_ref=slots_ref.at[yt, :, ct, :, pl.ds(half, half)], dst_ref=self.r1r.at[:, q_col], send_sem=self.s1.at[1, i], recv_sem=self.v1.at[1, i], device_id=dev(side, yt, x, ct), device_id_type=MESH_ID))
+        self.own = [pltpu.make_async_copy(slots_ref.at[:, x, core, :, pl.ds(0, half)], self.r1l.at[:, q_row], self.loc.at[0]),
+                    pltpu.make_async_copy(slots_ref.at[y, :, core, :, pl.ds(half, half)], self.r1r.at[:, q_col], self.loc.at[1])]
+        for i in range(1, side):
+            yt, xt = (y + i) % side, (x + i) % side
+            self.second_l.append(pltpu.make_async_remote_copy(src_ref=self.ps_l.at[yt], dst_ref=self.p2l.at[i - 1], send_sem=self.s2.at[0, i], recv_sem=self.v2.at[0, i], device_id=dev(side, yt, x, core), device_id_type=MESH_ID))
+            self.second_r.append(pltpu.make_async_remote_copy(src_ref=self.ps_r.at[xt], dst_ref=self.p2r.at[i - 1], send_sem=self.s2.at[1, i], recv_sem=self.v2.at[1, i], device_id=dev(side, y, xt, core), device_id_type=MESH_ID))
+
+    def launch(self):
+        start(self.first)
+        start(self.own)
+
+    def selector(self, ids):
+        wide = self.meta.shape[-1]
         src = lax.broadcasted_iota(jnp.int32, (wide, wide), 0)
         dst = lax.broadcasted_iota(jnp.int32, (wide, wide), 1)
         hit = jnp.zeros((wide, wide), F32)
         for q, e in enumerate(ids):
-            hit = jnp.where((src == offset + e) & (dst == q), 1.0, hit)
-            hit = jnp.where((src == offset + experts + e) & (dst == peers + q), 1.0, hit)
+            hit = jnp.where((src == self.offset + e) & (dst == q), 1.0, hit)
+            hit = jnp.where((src == self.offset + self.experts + e) & (dst == self.peers + q), 1.0, hit)
         return hit.astype(BF16)
 
-    sel_l, sel_r = selector(row_ids), selector(col_ids)
-
-    def partial(block, sel, landed, sums, k):
+    def partial(self, block, sel, landed, sums, k):
+        lane = lax.broadcasted_iota(jnp.int32, (1, self.slots), 1).astype(F32) + 1.0
         table = jnp.dot(block, sel, preferred_element_type=F32)
         weights = []
-        for q in range(peers):
-            scale = table[:, peers + q:peers + q + 1] if gated else 1.0
+        for q in range(self.peers):
+            scale = table[:, self.peers + q:self.peers + q + 1] if self.gated else 1.0
             weights.append(jnp.where(table[:, q:q + 1] == lane, scale, 0.0).astype(BF16))
-        vals = landed[k].reshape(peers * slots, half)
+        vals = landed[k].reshape(self.peers * self.slots, self.half)
         sums[k] = jnp.dot(jnp.concatenate(weights, axis=1), vals, preferred_element_type=F32)
 
-    def sum_l(i):
-        k = (y + i) % side
-        partial(meta[k, x, core], sel_l, r1l, ps_l, k)
-
-    def sum_r(i):
-        k = (x + i) % side
-        partial(meta[y, k, core], sel_r, r1r, ps_r, k)
-
-    def send_l(i):
-        yt = (y + i) % side
-        return pltpu.make_async_remote_copy(src_ref=ps_l.at[yt], dst_ref=p2l.at[i], send_sem=s2.at[0, i], recv_sem=v2.at[0, i], device_id=dev(side, yt, x, core), device_id_type=MESH_ID)
-
-    def send_r(i):
-        xt = (x + i) % side
-        return pltpu.make_async_remote_copy(src_ref=ps_r.at[xt], dst_ref=p2r.at[i], send_sem=s2.at[1, i], recv_sem=v2.at[1, i], device_id=dev(side, y, xt, core), device_id_type=MESH_ID)
-
-    second = []
-    for i in range(1, side):
-        sum_l(i)
-        if i > 1:
-            second.append(send_r(i - 1))
-            second[-1].start()
-        sum_r(i)
-        second.append(send_l(i))
-        second[-1].start()
-    sum_l(0)
-    second.append(send_r(side - 1))
-    second[-1].start()
-    sum_r(0)
-    sent(first)
-    arrive(second)
-    total_l = base_ref[:, :half].astype(F32) + ps_l[y]
-    for i in range(1, side):
-        total_l = total_l + p2l[i]
-    out_ref[:, :half] = total_l.astype(BF16)
-    total_r = base_ref[:, half:].astype(F32) + ps_r[x]
-    for i in range(1, side):
-        total_r = total_r + p2r[i]
-    out_ref[:, half:] = total_r.astype(BF16)
-    sent(second)
-
-
-def run_combine(ident, out_slots, base, meta, offset, gated, forward, head_dim, extra):
+    def sum_and_send(self):
+        _, y, x, core = self.spot
+        side = self.side
+        for copy in self.own:
+            copy.wait()
+        arrive(self.first)
+        sel_l = self.selector([y * self.peers + q for q in range(self.peers)])
+        sel_r = self.selector([((q // CORES) * side + x) * CORES + q % CORES for q in range(self.peers)])
+        for i in range(1, side + 1):
+            ky, kx = (y + i) % side, (x + i) % side
+            self.partial(self.meta[ky, x, core], sel_l, self.r1l, self.ps_l, ky)
+            if i > 1:
+                self.second_r[i - 2].start()
+            self.partial(self.meta[y, kx, core], sel_r, self.r1r, self.ps_r, kx)
+            if i < side:
+                self.second_l[i - 1].start()
+
+    def total(self, base, out_ref):
+        _, y, x, core = self.spot
+        half = self.half
+        arrive(self.second_l + self.second_r)
+        for cols, sums, k, landed in ((slice(0, half), self.ps_l, y, self.p2l), (slice(half, 2 * half), self.ps_r, x, self.p2r)):
+            total = sums[k] if base is None else base[:, cols].astype(F32) + sums[k]
+            for i in range(1, self.side):
+                total = total + landed[i - 1]
+            out_ref[:, cols] = total.astype(BF16)
+
+    def drain(self):
+        sent(self.first + self.second_l + self.second_r)
+
+
+def return_moves(side):
+    return [(k, dc) for k in range(1, side) for dc in range(CORES)] + [(0, 1)]
+
+
+RETURN_BUFFERS = 6
+
+
+def return_kernel(side, experts, head_dim, slots_b, u_all, meta_ref, w1_ref, w2_ref, w3_ref, h_ref, x_ref, dy_ref, gains_ref, wq, wk, wv, wo, y_ref, dx_ref, gq, gk, gv, go, gn, fwd_ref, meta, w13, w2, utile, recv, otile, du_s, *rest):
+    bufs_b, bufs_a, rest = rest[:RETURN_BUFFERS], rest[RETURN_BUFFERS:2 * RETURN_BUFFERS], rest[2 * RETURN_BUFFERS:]
+    att, rest = rest[:11], rest[11:]
+    sems_b, sems_a, (loc, tin, tout) = rest[:5], rest[5:10], rest[10:]
+    me, y, x, core = place_of(side)
+    partners = [(y, (x + k) % side, (core + dc) % CORES) for k, dc in return_moves(side)]
+    partners += [((y + k) % side, x, (core + dc) % CORES) for k, dc in return_moves(side) if k]
+    greet([dev(side, *spot) for spot in partners])
+    back_b = Return(side, experts, 2 * experts, False, slots_b, meta, bufs_b, sems_b)
+    back_a = Return(side, experts, 0, True, fwd_ref, meta, bufs_a, sems_a)
+    back_b.launch()
+    width = w2_ref.shape[0]
+    slots = fwd_ref.shape[3]
+    dim = x_ref.shape[-1]
+    loads = [pltpu.make_async_copy(meta_ref, meta, loc.at[0]), pltpu.make_async_copy(w2_ref, w2, loc.at[1]),
+             pltpu.make_async_copy(w1_ref, w13.at[:, pl.ds(0, width)], loc.at[2]), pltpu.make_async_copy(w3_ref, w13.at[:, pl.ds(width, width)], loc.at[3])]
+    start(loads)
+    steps = side * side
+    spot = lax.broadcasted_iota(jnp.int32, (slots, 1), 0).astype(F32) + 1.0
+
+    def fetch(g, slot):
+        return pltpu.make_async_copy(u_all.at[g // side, g % side], utile.at[slot], tin.at[slot])
+
+    def put(g, slot):
+        return pltpu.make_async_copy(otile.at[slot], fwd_ref.at[g // side, g % side], tout.at[slot])
+
+    fetch(0, 0).start()
+    for copy in loads:
+        copy.wait()
+
+    def step(g, carry):
+        slot = g % 2
+        fetch(g, slot).wait()
+
+        @pl.when(g + 1 < steps)
+        def _():
+            fetch(g + 1, 1 - slot).start()
+        for j in range(CORES):
+            lines = my_rows(meta[g // side, g % side, j], experts, me, 0)
+            pick = jnp.where(lines[0:1] == spot, 1.0, 0.0).astype(BF16)
+            recv[pl.ds(j * slots, slots), :] = jnp.dot(pick, utile[slot, j], preferred_element_type=F32).astype(BF16)
+        act = jnp.dot(recv[...], w13[...], preferred_element_type=F32).astype(BF16).astype(F32)
+        act_1, act_3 = act[:, :width], act[:, width:]
+        hidden = (act_1 * jax.nn.sigmoid(act_1) * act_3).astype(BF16)
+
+        @pl.when(g >= 2)
+        def _():
+            put(g - 2, slot).wait()
+        otile[slot] = jnp.dot(hidden, w2[...], preferred_element_type=F32).astype(BF16).reshape(CORES, slots, dim)
+        put(g, slot).start()
+        return carry
+
+    lax.fori_loop(0, steps, step, 0)
+    put(steps - 2, steps % 2).wait()
+    put(steps - 1, 1 - steps % 2).wait()
+    back_a.launch()
+    q_s, k_s, v_s, ctx_s, normed_s = att[:5]
+    attn = attention_rows(x_ref, gains_ref[0:1].astype(F32), wq, wk, wv, wo, head_dim, q_s, k_s, v_s, ctx_s, normed_s)
+    att[10][...] = (x_ref[...].astype(F32) + attn.astype(BF16).astype(F32)).astype(BF16)
+    back_b.sum_and_send()
+    back_a.sum_and_send()
+    back_b.total(None, du_s)
+    attention_backward(head_dim, x_ref, dy_ref, du_s, gains_ref, wq, wk, wv, wo, dx_ref, gq, gk, gv, go, gn, *att)
+    back_a.total(h_ref, y_ref)
+    back_b.drain()
+    back_a.drain()
+
+
+def run_returns(slots_b, u_all, meta, experts_w, h_a, x_b, dy_b, gains, flat, head_dim, group):
     side = meta.shape[0]
-    group, capacity, dim = out_slots.shape
-    rows = base.shape[0]
+    capacity, dim = slots_b.shape[1:]
+    rows = x_b.shape[0]
     half = dim // 2
     peers = side * CORES
-    cube = out_slots.reshape(side, side, CORES, capacity, dim)
+    width = experts_w[1].shape[0]
+    full, kv = flat[0].shape[1], flat[1].shape[1]
     any_spec, vmem = pl.BlockSpec(memory_space=pl.ANY), pl.BlockSpec(memory_space=pltpu.VMEM)
-    out_shape = [jax.ShapeDtypeStruct(base.shape, BF16)]
-    in_specs = [any_spec, vmem, any_spec]
-    out_specs = [vmem]
-    scratch = [
-        pltpu.VMEM(meta.shape, BF16),
-        pltpu.VMEM((side, peers, capacity, half), BF16),
-        pltpu.VMEM((side, peers, capacity, half), BF16),
-        pltpu.VMEM((side, rows, half), F32),
-        pltpu.VMEM((side, rows, half), F32),
-        pltpu.VMEM((side, rows, half), F32),
-        pltpu.VMEM((side, rows, half), F32),
-        pltpu.SemaphoreType.DMA((3,)),
-        pltpu.SemaphoreType.DMA((2, peers)),
-        pltpu.SemaphoreType.DMA((2, peers)),
-        pltpu.SemaphoreType.DMA((2, side)),
-        pltpu.SemaphoreType.DMA((2, side)),
-    ]
-    if forward:
-        in_specs += [any_spec, vmem, vmem, vmem]
-        out_specs += [any_spec]
-        out_shape += [jax.ShapeDtypeStruct(out_slots.shape, BF16)]
-        scratch += [
-            pltpu.VMEM((2, BLOCKS, rows, dim), BF16),
-            pltpu.VMEM((BLOCKS * capacity, dim), BF16),
-            pltpu.VMEM((2, BLOCKS, capacity, dim), BF16),
-            pltpu.VMEM((dim, 2 * extra[2].shape[0]), BF16),
-            pltpu.SemaphoreType.DMA((2,)),
-            pltpu.SemaphoreType.DMA((2,)),
-        ]
-    else:
-        in_specs += [vmem] * len(extra)
-        out_specs += [vmem] * 6
-        full, kv = extra[4].shape[1], extra[5].shape[1]
-        out_shape += [jax.ShapeDtypeStruct(base.shape, BF16)] + [jax.ShapeDtypeStruct(part.shape, BF16) for part in extra[4:]] + [jax.ShapeDtypeStruct((2, dim), F32)]
-        scratch += [pltpu.VMEM((rows, cols), BF16) for cols in (full, kv, kv, full, dim, full, full, kv, kv, dim)]
+    cube = slots_b.reshape(side, side, CORES, capacity, dim)
+    sets = [pltpu.VMEM((side, peers, capacity, half), BF16)] * 2 + [pltpu.VMEM((side, rows, half), F32)] * 2 + [pltpu.VMEM((side - 1, rows, half), F32)] * 2
+    sems = [pltpu.SemaphoreType.DMA((2,)), pltpu.SemaphoreType.DMA((2, peers)), pltpu.SemaphoreType.DMA((2, peers)), pltpu.SemaphoreType.DMA((2, side)), pltpu.SemaphoreType.DMA((2, side))]
     return pl.pallas_call(
-        functools.partial(combine_kernel, side, group, offset, gated, forward, head_dim),
-        out_shape=out_shape,
-        in_specs=in_specs,
-        out_specs=out_specs,
-        scratch_shapes=scratch,
-        compiler_params=pltpu.CompilerParams(collective_id=ident, has_side_effects=True, vmem_limit_bytes=64000000),
-    )(cube, base, meta, *extra)
+        functools.partial(return_kernel, side, group, head_dim),
+        out_shape=[jax.ShapeDtypeStruct(x_b.shape, BF16)] * 2 + [jax.ShapeDtypeStruct(part.shape, BF16) for part in flat] + [jax.ShapeDtypeStruct((2, dim), F32), jax.ShapeDtypeStruct(cube.shape, BF16)],
+        in_specs=[any_spec] * 6 + [vmem] * 8,
+        out_specs=[vmem] * 7 + [any_spec],
+        scratch_shapes=[
+            pltpu.VMEM(meta.shape, BF16),
+            pltpu.VMEM((dim, 2 * width), BF16),
+            pltpu.VMEM((width, dim), BF16),
+            pltpu.VMEM((2, CORES, rows, dim), BF16),
+            pltpu.VMEM((CORES * capacity, dim), BF16),
+            pltpu.VMEM((2, CORES, capacity, dim), BF16),
+            pltpu.VMEM((rows, dim), BF16),
+        ] + sets + sets + [pltpu.VMEM((rows, cols), BF16) for cols in (full, kv, kv, full, dim, full, full, kv, kv, dim, dim)] + sems + sems + [pltpu.SemaphoreType.DMA((4,)), pltpu.SemaphoreType.DMA((2,)), pltpu.SemaphoreType.DMA((2,))],
+        compiler_params=pltpu.CompilerParams(collective_id=1, has_side_effects=True, vmem_limit_bytes=67043328),
+    )(cube, u_all, meta, *experts_w, h_a, x_b, dy_b, gains, *flat)
 
 
 def solution(mesh):
     group = mesh.shape['expert']
 
     def local_step(x_a, x_b, dy_b, eid_a, slot_a, gate_a, eid_b, slot_b, gate_b, u_b, norm_1, norm_2, w_q, w_k, w_v, w_o, w_1, w_2, w_3):
-        experts = w_1.shape[0] * group
         rows, model_dim = x_a.shape
         w1, w2, w3 = w_1[0], w_2[0], w_3[0]
 
@@ -629,8 +604,7 @@
         flat = (w_q.reshape(model_dim, -1), w_k.reshape(model_dim, -1), w_v.reshape(model_dim, -1), w_o.reshape(-1, model_dim))
 
         u_all, meta, grad_in, grad_w1, grad_w2, grad_w3, h_a = run_backward(dy_b, x_a, routes, u_b[0], (w1, w2, w3, gains) + flat, head_dim, group)
-        du, out_a = run_combine(1, grad_in, jnp.zeros_like(x_b), meta, 2 * experts, False, True, head_dim, (u_all.reshape(group, rows, model_dim), w1, w2, w3))
-        y_a, dx_b, g_q, g_k, g_v, g_o, g_n = run_combine(2, out_a, h_a, meta, 0, True, False, head_dim, (x_b, dy_b, du, gains) + flat)
+        y_a, dx_b, g_q, g_k, g_v, g_o, g_n, _ = run_returns(grad_in, u_all, meta, (w1, w2, w3), h_a, x_b, dy_b, gains, flat, head_dim, group)
         grads = tuple(g.reshape(w.shape).astype(F32)[None] for g, w in ((g_q, w_q), (g_k, w_k), (g_v, w_v), (g_o, w_o))) + (g_n[0:1], g_n[1:2])
         return (y_a, dx_b, grad_w1[None], grad_w2[None], grad_w3[None], *grads)
 

time: 340 us -> 312 us (0.918); the launches traced: 334 us -> 312 us
  Pallas kernels: 303 us -> 283 us
    pallas_call x2 -> x1, Pallas kernels: 167 us -> 147 us  [run_returns(): pl.pallas_call(functools.partial(return_kernel, side, group, head_dim), o...]
where the time goes in v4:
time: 312 us
  Pallas kernels  283 us (91%)
  local copies, waits for them, and re-layouts  25.2 us (8%)
    pallas_call x1, Pallas kernels, run_returns(): pl.pallas_call(functools.partial(return_kernel, side, group, head_dim), o...  147 us
    pallas_call x1, Pallas kernels, run_backward(): pl.pallas_call(functools.partial(backward_kernel, side, group, head_dim),...  136 us
    convert_element_type x3, local copies, waits for them, and re-layouts, local_step(): g.reshape(w.shape).astype(F32)[None]  8.43 us
    unnamed x23, local copies, waits for them, and re-layouts  7.63 us

profile of v4, /device:TPU:97, one launch (start us, length us, event | category | flops | bytes accessed | tf_op | source)
XLA Modules:
  0.0 311.7 jit_solution(5549039740228677638)
XLA Ops:
  0.6 0.0 copy-start.6
  0.7 0.8 stack.9
  1.4 0.7 stack.10
  2.1 0.6 pad_maximum_fusion.gains_ref
  2.7 2.4 copy.37.wk_ref.wk
  5.1 1.3 copy.38.wv_ref.wv
  6.5 2.5 copy.36.wq_ref.wq
  9.0 136.1 %shard_map.266 = (bf16[4,4,2,256,1024]{4,3,2,1,0:T(8,128)(2,1)}, bf16[4,4,2,256,128]{4,3,2,1,0:T(8,128)(2,1)}, bf16[32,128,1024]{2,1,0:T(8,128)(2,1)}, f32[1024,...) custom-call(bf16[256,1024]{1,0:T(8,128)(2,1)} %dy_ref.3, ...), custom_call_target="tpu_custom_call" | custom-call | tf_op jit(solution)/shard_map/pallas_call | solution.py:381
  145.1 146.6 %shard_map.267 = (bf16[256,1024]{1,0:T(8,128)(2,1)}, bf16[256,1024]{1,0:T(8,128)(2,1)}, bf16[1024,1024]{1,0:T(8,128)(2,1)}, bf16[1024,512]{1,0:T(8,128)(2,1)}, b...) custom-call(bf16[4,4,2,128,1024]{4,3,2,1,0:T(8,128)(2,1)} %bitcast.2, ...), custom_call_target="tpu_custom_call" | custom-call | tf_op jit(solution)/shard_map/pallas_call | solution.py:576
  291.8 1.4 fusion
  293.2 2.6 copy.43
  295.8 1.6 copy.44
  297.4 4.3 %copy.42 = f32[1024,1024]{0,1:T(8,128)} copy(bf16[1024,1024]{1,0:T(8,128)(2,1)} %get-tuple-element.34) | data formatting | bytes 6291456 | tf_op jit(solution)/shard_map/convert_element_type | solution.py:608
  301.6 0.0 copy-start.4
  301.6 2.5 convert.4
  304.1 0.8 copy.50
  304.9 0.0 copy-done.7
  304.9 0.8 copy.51
  305.7 0.0 copy-done.4
  305.7 1.3 copy.52
  307.0 1.0 copy-done.3
  308.1 1.3 copy.53
  309.4 1.0 copy-done.2
  310.4 1.3 copy.54
  (12 shorter events, 0.0 us)
Async XLA Ops:
  0.6 4.5 %copy-start.6 = (bf16[1024,8,64]{0,2,1:T(8,128)(2,1)S(1)}, bf16[1024,8,64]{0,2,1:T(8,128)(2,1)}, u32[]{:S(2)}) copy-start(bf16[1024,8,64]{0,2,1:T(8,128)(2,1)} %param.33) | copy-start | bytes 3145732
  2.7 3.7 %copy-start.1 = (bf16[1024,16,64]{0,2,1:T(8,128)(2,1)S(1)}, bf16[1024,16,64]{0,2,1:T(8,128)(2,1)}, u32[]{:S(2)}) copy-start(bf16[1024,16,64]{0,2,1:T(8,128)(2,1)} %param.31) | copy-start | bytes 6291460
  291.8 4.0 %copy-start.5 = (bf16[1024,512]{1,0:T(8,128)(2,1)S(1)}, bf16[1024,512]{1,0:T(8,128)(2,1)}, u32[]{:S(2)}) copy-start(bf16[1024,512]{1,0:T(8,128)(2,1)} %get-tuple-element.36) | copy-start | bytes 3145732
  297.4 4.3 %copy-start = (bf16[1024,1024]{1,0:T(8,128)(2,1)S(1)}, bf16[1024,1024]{1,0:T(8,128)(2,1)}, u32[]{:S(2)}) copy-start(bf16[1024,1024]{1,0:T(8,128)(2,1)} %get-tuple-element.37) | copy-start | bytes 6291460
  301.6 2.5 copy-start.8
  301.6 3.3 %copy-start.7 = (bf16[256,1024]{1,0:T(8,128)(2,1)S(1)}, bf16[256,1024]{1,0:T(8,128)(2,1)}, u32[]{:S(2)}) copy-start(bf16[256,1024]{1,0:T(8,128)(2,1)} %get-tuple-element.64) | copy-start | bytes 1572868
  301.6 4.1 %copy-start.4 = (f32[1024,512]{1,0:T(8,128)S(1)}, f32[1024,512]{1,0:T(8,128)}, u32[]{:S(2)}) copy-start(f32[1024,512]{1,0:T(8,128)} %get-tuple-element.31) | copy-start | bytes 6291460
  305.7 2.3 copy-start.3
  308.1 2.3 copy-start.2

commit v5 on v4

--- a/solution.py
+++ b/solution.py
@@ -242,7 +242,7 @@
 BLOCKS = 4
 
 
-def backward_kernel(side, experts, head_dim, dy_ref, x_ref, eid_a, slot_a, gate_a, eid_b, slot_b, gate_b, ub_ref, w1_ref, w2_ref, w3_ref, gains_ref, wq_ref, wk_ref, wv_ref, wo_ref, u_all, meta_all, du_ref, gw1, gw2, gw3, h_ref, buf, w13, w13t, w2t, tile, dout, acts, dtile, u_ref, loc, tin, tout, sa, ra, sb, rb):
+def backward_kernel(side, experts, head_dim, dy_ref, x_ref, eid_a, slot_a, gate_a, eid_b, slot_b, gate_b, ub_ref, w1_ref, w2_ref, w3_ref, gains_ref, wq_ref, wk_ref, wv_ref, wo_ref, u_all, meta_all, du_ref, gw1, gw2, gw3, h_ref, buf, w13, w13t, w2t, tile, pre_s, dout, acts, dtile, u_ref, loc, tin, tout, sa, ra, sb, rb):
     me, y, x, core = place_of(side)
     partners = [dev(side, y, (x + k) % side, core) for k in range(1, side)]
     partners += [dev(side, (y + k) % side, x, core) for k in range(1, side)]
@@ -273,13 +273,6 @@
     gw1[...] = jnp.zeros_like(gw1)
     gw2[...] = jnp.zeros_like(gw2)
     gw3[...] = jnp.zeros_like(gw3)
-    own_u.wait()
-    second.owns()
-    first.relays((0, 1, 3, 2))
-    start(second.line[0])
-    first.rest_of_lines()
-    arrive(first.twin_own + first.twin_line)
-
     slots = du_ref.shape[1]
     group = du_ref.shape[0]
     rows = BLOCKS * slots
@@ -298,17 +291,40 @@
     def put(g, slot):
         return pltpu.make_async_copy(dtile.at[slot], du_ref.at[pl.ds(turn(g) * BLOCKS, BLOCKS)], tout.at[slot])
 
+    spot = lax.broadcasted_iota(jnp.int32, (slots, 1), 0).astype(F32) + 1.0
+
+    def warm(g, carry):
+        slot = g % 2
+
+        @pl.when(g == 4)
+        def _():
+            first.relays((0, 1))
+        fetch(g, slot).wait()
+
+        @pl.when(g + 1 < steps)
+        def _():
+            fetch(g + 1, 1 - slot).start()
+        pre_s[pl.ds(g * rows, rows), :] = jnp.dot(tile[slot], w13[...], preferred_element_type=F32).astype(BF16)
+        return carry
+
     fetch(0, 0).start()
-    spot = lax.broadcasted_iota(jnp.int32, (slots, 1), 0).astype(F32) + 1.0
+    own_u.wait()
+    lax.fori_loop(0, steps, warm, 0)
+    fetch(0, 0).start()
+    first.relays((3, 2))
+    second.owns()
+    start(second.line[0])
+    first.rest_of_lines()
+    arrive(first.twin_own + first.twin_line)
 
     def step(g, carry):
         slot = g % 2
 
+        @pl.when(g == 3)
+        def _():
+            second.lines()
+
         @pl.when(g == 1)
-        def _():
-            second.lines()
-
-        @pl.when(g == 2)
         def _():
             first.fars()
 
@@ -334,7 +350,7 @@
             lines = my_rows(block[:, dim:], experts, me, 2 * experts)
             pick = jnp.where(lines[0:1] == spot, lines[1:2], 0.0).astype(BF16)
             dout[pl.ds(j * slots, slots), :] = jnp.dot(pick, block[:, :dim], preferred_element_type=F32).astype(BF16)
-        pre = jnp.dot(tile[slot], w13[...], preferred_element_type=F32).astype(BF16).astype(F32)
+        pre = pre_s[pl.ds(g * rows, rows), :].astype(F32)
         pre_1, pre_3 = pre[:, :width], pre[:, width:]
         sigma = jax.nn.sigmoid(pre_1)
         silu_1 = pre_1 * sigma
@@ -397,6 +413,7 @@
             pltpu.VMEM((2 * width, dim), BF16),
             pltpu.VMEM((dim, width), BF16),
             pltpu.VMEM((2, tall, dim), BF16),
+            pltpu.VMEM((group * slots, 2 * width), BF16),
             pltpu.VMEM((tall, dim), BF16),
             pltpu.VMEM((tall, 2 * width), BF16),
             pltpu.VMEM((2, BLOCKS, slots, dim), BF16),
@@ -405,7 +422,7 @@
             pltpu.SemaphoreType.DMA((2,)),
             pltpu.SemaphoreType.DMA((2,)),
         ] + [pltpu.SemaphoreType.DMA((GATHER_COPIES,))] * 4,
-        compiler_params=pltpu.CompilerParams(collective_id=0, has_side_effects=True, vmem_limit_bytes=64000000),
+        compiler_params=pltpu.CompilerParams(collective_id=0, has_side_effects=True, vmem_limit_bytes=67043328),
     )(dy, x_a, *routes, saved, *weights)
 
 
@@ -463,14 +480,14 @@
         arrive(self.first)
         sel_l = self.selector([y * self.peers + q for q in range(self.peers)])
         sel_r = self.selector([((q // CORES) * side + x) * CORES + q % CORES for q in range(self.peers)])
-        for i in range(1, side + 1):
+        def both(i, carry):
             ky, kx = (y + i) % side, (x + i) % side
             self.partial(self.meta[ky, x, core], sel_l, self.r1l, self.ps_l, ky)
-            if i > 1:
-                self.second_r[i - 2].start()
             self.partial(self.meta[y, kx, core], sel_r, self.r1r, self.ps_r, kx)
-            if i < side:
-                self.second_l[i - 1].start()
+            return carry
+
+        lax.fori_loop(1, side + 1, both, 0)
+        start(self.second_l + self.second_r)
 
     def total(self, base, out_ref):
         _, y, x, core = self.spot

time: 312 us -> 302 us (0.968)
  Pallas kernels: 283 us -> 272 us
    pallas_call x1, Pallas kernels: 136 us -> 126 us  [run_backward(): pl.pallas_call(functools.partial(backward_kernel, side, group, head_dim),...]
where the time goes in v5:
time: 302 us; the launch traced here: 301 us
  Pallas kernels  272 us (90%)
  local copies, waits for them, and re-layouts  25.2 us (8%)
  other arithmetic  3.09 us (1%)
    pallas_call x1, Pallas kernels, run_returns(): pl.pallas_call(functools.partial(return_kernel, side, group, head_dim), o...  147 us
    pallas_call x1, Pallas kernels, run_backward(): pl.pallas_call(functools.partial(backward_kernel, side, group, head_dim),...  126 us
    convert_element_type x3, local copies, waits for them, and re-layouts, local_step(): g.reshape(w.shape).astype(F32)[None]  8.43 us
    unnamed x23, local copies, waits for them, and re-layouts  7.63 us

profile of v5, /device:TPU:97, one launch (start us, length us, event | category | flops | bytes accessed | tf_op | source)
XLA Modules:
  0.0 301.5 jit_solution(1117994428051577796)
XLA Ops:
  0.7 0.8 stack.9
  1.4 0.7 stack.10
  2.1 0.6 pad_maximum_fusion.gains_ref
  2.7 2.4 copy.37.wk_ref.wk
  5.1 1.3 copy.38.wv_ref.wv
  6.5 0.0 copy-done.1
  6.5 2.5 copy.36.wq_ref.wq
  9.0 125.7 %shard_map.266 = (bf16[4,4,2,256,1024]{4,3,2,1,0:T(8,128)(2,1)}, bf16[4,4,2,256,128]{4,3,2,1,0:T(8,128)(2,1)}, bf16[32,128,1024]{2,1,0:T(8,128)(2,1)}, f32[1024,...) custom-call(bf16[256,1024]{1,0:T(8,128)(2,1)} %dy_ref.3, ...), custom_call_target="tpu_custom_call" | custom-call | tf_op jit(solution)/shard_map/pallas_call | solution.py:397
  134.7 146.8 %shard_map.267 = (bf16[256,1024]{1,0:T(8,128)(2,1)}, bf16[256,1024]{1,0:T(8,128)(2,1)}, bf16[1024,1024]{1,0:T(8,128)(2,1)}, bf16[1024,512]{1,0:T(8,128)(2,1)}, b...) custom-call(bf16[4,4,2,128,1024]{4,3,2,1,0:T(8,128)(2,1)} %bitcast.2, ...), custom_call_target="tpu_custom_call" | custom-call | tf_op jit(solution)/shard_map/pallas_call | solution.py:593
  281.5 1.4 fusion
  282.9 2.6 copy.43
  285.5 1.6 copy.44
  287.1 4.3 %copy.42 = f32[1024,1024]{0,1:T(8,128)} copy(bf16[1024,1024]{1,0:T(8,128)(2,1)} %get-tuple-element.34) | data formatting | bytes 6291456 | tf_op jit(solution)/shard_map/convert_element_type | solution.py:625
  291.4 0.0 copy-start.4
  291.4 2.5 convert.4
  293.9 0.8 copy.50
  294.6 0.0 copy-done.7
  294.7 0.8 copy.51
  295.4 0.0 copy-done.4
  295.5 1.3 copy.52
  296.8 1.0 copy-done.3
  297.8 1.3 copy.53
  299.1 1.0 copy-done.2
  300.1 1.3 copy.54
  (12 shorter events, 0.0 us)
Async XLA Ops:
  0.6 4.5 %copy-start.6 = (bf16[1024,8,64]{0,2,1:T(8,128)(2,1)S(1)}, bf16[1024,8,64]{0,2,1:T(8,128)(2,1)}, u32[]{:S(2)}) copy-start(bf16[1024,8,64]{0,2,1:T(8,128)(2,1)} %param.33) | copy-start | bytes 3145732
  2.7 3.7 %copy-start.1 = (bf16[1024,16,64]{0,2,1:T(8,128)(2,1)S(1)}, bf16[1024,16,64]{0,2,1:T(8,128)(2,1)}, u32[]{:S(2)}) copy-start(bf16[1024,16,64]{0,2,1:T(8,128)(2,1)} %param.31) | copy-start | bytes 6291460
  281.5 4.0 %copy-start.5 = (bf16[1024,512]{1,0:T(8,128)(2,1)S(1)}, bf16[1024,512]{1,0:T(8,128)(2,1)}, u32[]{:S(2)}) copy-start(bf16[1024,512]{1,0:T(8,128)(2,1)} %get-tuple-element.36) | copy-start | bytes 3145732
  287.1 4.3 %copy-start = (bf16[1024,1024]{1,0:T(8,128)(2,1)S(1)}, bf16[1024,1024]{1,0:T(8,128)(2,1)}, u32[]{:S(2)}) copy-start(bf16[1024,1024]{1,0:T(8,128)(2,1)} %get-tuple-element.37) | copy-start | bytes 6291460
  291.4 2.5 copy-start.8
  291.4 3.3 %copy-start.7 = (bf16[256,1024]{1,0:T(8,128)(2,1)S(1)}, bf16[256,1024]{1,0:T(8,128)(2,1)}, u32[]{:S(2)}) copy-start(bf16[256,1024]{1,0:T(8,128)(2,1)} %get-tuple-element.64) | copy-start | bytes 1572868
  291.4 4.1 %copy-start.4 = (f32[1024,512]{1,0:T(8,128)S(1)}, f32[1024,512]{1,0:T(8,128)}, u32[]{:S(2)}) copy-start(f32[1024,512]{1,0:T(8,128)} %get-tuple-element.31) | copy-start | bytes 6291460
  295.4 2.3 copy-start.3
  297.8 2.3 copy-start.2
